TPU v7x, 32 devices: a whole 2x2x4 slice. The times are simulated.
32 devices in a mesh: row: 8 (over z, x), col: 4 (over y, core).
Axes of the slice: x: 2, y: 2, z: 4, core: 2. Of those that a mesh axis runs over, the one named last changes fastest.
Arguments:
- voltage: float32 [2, 4096, 16384], P(None, ('row', 'col')), may hold values from -6 to 6
- chirp_phase: float32 [16384, 4096], P(('row', 'col')), may hold values from -3.140625 to 3.140625
- filter_taps: float32 [8, 1024], replicated, may hold values from -0.0625 to 0.0625
Outputs:
- filterbank: float32 [2, 1024, 65536], P(None, None, ('row', 'col'))
All inputs are finite; a program needn't handle non-finite values.
Results may differ from a plain program's by a relative error of at most 0.00015.
Values sent between devices are 32-bit elements; how exact they have to be, the bound alone decides.
No kernel may reach another device: no remote copies, remote signals or barrier semaphores. Data moves between devices by JAX's collectives and lax.ppermute only.
A program may use at most 192 MiB of HBM per device.

v0:
```python
import math

import jax
import jax.numpy as jnp
from jax import lax
from jax.sharding import PartitionSpec as P

precise = lax.Precision.HIGHEST


def passed_along(block, axis, distance):
    devices = range(lax.axis_size(axis))
    route = [(i - distance, i) for i in devices if i - distance in devices]
    return lax.ppermute(block, axis, route)


def dft_table(radix, direction):
    digits = jnp.arange(radix, dtype=jnp.int32)
    product = digits[:, None] * digits[None, :] % radix
    turn = direction * 2.0 * math.pi / radix * product.astype(jnp.float32)
    cos_part = jnp.cos(turn)
    sin_part = jnp.sin(turn)
    upper = jnp.stack([cos_part, sin_part], axis=1)
    lower = jnp.stack([-sin_part, cos_part], axis=1)
    return jnp.stack([upper, lower], axis=0)


def complex_product(values, cos_part, sin_part):
    real_part = values[0] * cos_part - values[1] * sin_part
    imag_part = values[0] * sin_part + values[1] * cos_part
    return jnp.stack([real_part, imag_part])


def inner_twist(outer_radix, inner_radix, direction):
    outer_digits = jnp.arange(outer_radix, dtype=jnp.int32)
    inner_digits = jnp.arange(inner_radix, dtype=jnp.int32)
    length = outer_radix * inner_radix
    product = outer_digits[:, None] * inner_digits[None, :] % length
    turn = direction * 2.0 * math.pi / length * product.astype(jnp.float32)
    return (jnp.cos(turn), jnp.sin(turn))


def dft_rows(values, direction):
    length = values.shape[1]
    column_count = values.shape[2]
    inner_radix = min(length, 128)
    outer_radix = length // inner_radix
    blocked = values.reshape(2, outer_radix, inner_radix, column_count)
    partial_value = jnp.einsum(
        "cadk,cabm->dkbm", dft_table(outer_radix, direction), blocked, precision=precise
    )
    cos_part, sin_part = inner_twist(outer_radix, inner_radix, direction)
    partial_value = complex_product(partial_value, cos_part[:, :, None], sin_part[:, :, None])
    result = jnp.einsum(
        "cbdq,ckbm->dqkm", dft_table(inner_radix, direction), partial_value, precision=precise
    )
    return result.reshape(2, length, column_count)


def dft_cols(values, direction):
    length = values.shape[2]
    row_count = values.shape[1]
    inner_radix = min(length, 128)
    outer_radix = length // inner_radix
    blocked = values.reshape(2, row_count, outer_radix, inner_radix)
    partial_value = jnp.einsum(
        "cadk,cmab->dmkb", dft_table(outer_radix, direction), blocked, precision=precise
    )
    cos_part, sin_part = inner_twist(outer_radix, inner_radix, direction)
    partial_value = complex_product(partial_value, cos_part, sin_part)
    result = jnp.einsum(
        "cbdq,cmkb->dmqk", dft_table(inner_radix, direction), partial_value, precision=precise
    )
    return result.reshape(2, row_count, length)


def rotate(values, row_index, col_index, total, direction, factor):
    product = row_index[:, None] * col_index[None, :] % total
    turn = direction * 2.0 * math.pi / total * product.astype(jnp.float32)
    return complex_product(values, factor * jnp.cos(turn), factor * jnp.sin(turn))


def spread(values):
    return lax.all_to_all(values, ("row", "col"), split_axis=2, concat_axis=1, tiled=True)


def collect(values):
    return lax.all_to_all(values, ("row", "col"), split_axis=1, concat_axis=2, tiled=True)


def local(voltage, chirp_phase, filter_taps):
    device_count = lax.axis_size("row") * lax.axis_size("col")
    device = lax.axis_index(("row", "col"))
    local_rows = voltage.shape[1]
    total_rows = local_rows * device_count
    total_cols = voltage.shape[2]
    local_cols = total_cols // device_count
    total = total_rows * total_cols
    signal = spread(voltage)
    signal = dft_rows(signal, -1.0)
    row_index = jnp.arange(total_rows, dtype=jnp.int32)
    col_index = device * local_cols + jnp.arange(local_cols, dtype=jnp.int32)
    signal = rotate(signal, row_index, col_index, total, -1.0, 1.0)
    signal = collect(signal)
    signal = dft_cols(signal, -1.0)
    turned_phase = jnp.transpose(chirp_phase)
    local_phase = lax.all_to_all(
        turned_phase, ("row", "col"), split_axis=0, concat_axis=1, tiled=True
    )
    signal = complex_product(signal, jnp.cos(local_phase), jnp.sin(local_phase))
    signal = dft_cols(signal, 1.0)
    row_index = device * local_rows + jnp.arange(local_rows, dtype=jnp.int32)
    col_index = jnp.arange(total_cols, dtype=jnp.int32)
    signal = rotate(signal, row_index, col_index, total, 1.0, 1.0 / total)
    signal = spread(signal)
    signal = dft_rows(signal, 1.0)
    signal = collect(signal)
    tap_count = filter_taps.shape[0]
    channel_count = filter_taps.shape[1]
    samples = signal.reshape(2, local_rows * total_cols)
    frame_count = samples.shape[1] // channel_count
    frames = samples.reshape(2, frame_count, channel_count)
    history = passed_along(frames[:, frame_count - tap_count + 1 :, :], ("row", "col"), 1)
    extended = jnp.concatenate([history, frames], axis=1)
    turned = jnp.transpose(extended, (0, 2, 1))
    weighted = jnp.zeros((2, channel_count, frame_count), jnp.float32)
    for tap_delay in range(tap_count):
        offset = tap_count - 1 - tap_delay
        weighted = (
            weighted
            + filter_taps[tap_delay][None, :, None] * turned[:, :, offset : offset + frame_count]
        )
    return dft_rows(weighted, -1.0)


def solution(mesh):
    in_specs = (P(None, ("row", "col"), None), P(("row", "col"), None), P())
    out_specs = P(None, None, ("row", "col"))
    return jax.shard_map(local, mesh=mesh, in_specs=in_specs, out_specs=out_specs, check_vma=False)
```

profile of v0, /device:TPU:8, one launch (start us, length us, event | category | flops | bytes accessed | tf_op | source)
XLA Modules:
  0.0 2393.1 jit_solution(8709069159866349502)
XLA Ops:
  0.0 24.9 %copy.169 = f32[2,128,16384]{1,0,2:T(2,128)} copy(f32[2,128,16384]{2,1,0:T(8,128)} %param.3) | data formatting | bytes 33554432 | tf_op args[0]
  40.1 353.4 %all-to-all-done = f32[2,128,16384]{1,0,2:T(2,128)} async-done(((f32[2,128,16384]{1,0,2:T(2,128)}), f32[2,128,16384]{1,0,2:T(2,128)}, u32[]{:S(2)}, u32[]{:S(2)}) %all-to-all-start) | async-done | bytes 16777248 | tf_op jit(solution)/shard_map/all_to_all | solution.py:84
  393.5 19.6 all-to-all-start.2
  414.2 20.2 copy.234
  434.4 21.7 fusion.71
  466.4 28.9 %fusion.59 = f32[2,128,32,512]{3,1,2,0:T(8,128)S(1)} fusion(f32[2,32,128,512]{3,1,2,0:T(8,128)S(1)} %pad_maximum_fusion, f32[1,128,2,128]{1,3,0,2:T(8,128)S(1)} %get-tuple-element.30, f32[1,128,2,128]{1,3,0,2:T(8,128)S(1)} %get-tuple-element.29), kind=kOutput, calls=%fused_computation.103 | convolution fusion | flops 12884967424 | bytes 33816576 | tf_op jit(solution)/shard_map/cbdq,ckbm->dqkm/dot_general | solution.py:54
  518.8 36.9 %fusion.51 = (f32[1,4096,512]{2,1,0:T(8,128)S(1)}, f32[1,4096,512]{2,1,0:T(8,128)S(1)}) fusion(f32[1,128,32,512]{3,2,1,0:T(8,128)S(1)} %copy.173, f32[1,128,32,512]{3,2,1,0:T(8,128)S(1)} %copy.172, s32[512]{0:T(512)S(1)} %iota_add_fusion), kind=kLoop, calls=%fused_computation.77 | loop fusion | flops 41943040 | bytes 33556480 | tf_op jit(solution)/shard_map/sub | solution.py:29
  557.6 32.2 %copy.174 = f32[2,4096,512]{2,0,1:T(2,128)} copy(f32[2,4096,512]{2,1,0:T(8,128)S(1)} %pad_maximum_fusion.1) | data formatting | bytes 33554432 | tf_op jit(solution)/shard_map/stack | solution.py:31
  607.9 31.5 %sine_bitcast_fusion = (f32[128,32,512]{2,0,1:T(8,128)}, f32[128,32,512]{2,0,1:T(8,128)}) fusion(f32[32,128,512]{2,1,0:T(8,128)} %all-to-all-done.2), kind=kLoop, calls=%fused_computation.93 | loop fusion | bytes 25165824 | tf_op jit(solution)/shard_map/sin | solution.py:110
  676.0 293.0 %all-to-all-done.1 = f32[2,4096,512]{2,0,1:T(2,128)} async-done(((f32[2,4096,512]{2,0,1:T(2,128)}), f32[2,4096,512]{2,0,1:T(2,128)}, u32[]{:S(2)}, u32[]{:S(2)}) %all-to-all-start.1) | async-done | bytes 16777248 | tf_op jit(solution)/shard_map/all_to_all | solution.py:88
  1000.7 18.1 copy.211
  1042.9 31.5 %fusion.36 = f32[2,128,128,128]{2,3,0,1:T(8,128)} fusion(f32[1,128,128,128]{2,3,0,1:T(8,128)} %get-tuple-element.14, f32[1,128,128,128]{2,3,0,1:T(8,128)} %get-tuple-element.13, f32[1,128,2,128]{1,3,0,2:T(8,128)S(1)} %get-tuple-element.30, f32[1,128,2,128]{1,3,0,2:T(8,128)S(1)} %get-tuple-element.29), kind=kOutput, calls=%fused_computation.59 | convolution fusion | flops 12889161728 | bytes 33816576 | tf_op jit(solution)/shard_map/cbdq,cmkb->dmqk/dot_general | solution.py:71
  1074.4 19.0 multiply_subtract_fusion.3
  1117.8 31.7 %fusion.40 = f32[2,128,128,128]{2,3,0,1:T(8,128)S(1)} fusion(f32[1,128,128,128]{2,3,0,1:T(8,128)} %get-tuple-element.12, f32[1,128,128,128]{2,3,0,1:T(8,128)} %get-tuple-element.11, f32[1,128,2,128]{1,3,2,0:T(8,128)S(1)} %get-tuple-element.28, f32[1,128,2,128]{1,3,2,0:T(8,128)S(1)} %get-tuple-element.27), kind=kOutput, calls=%fused_computation.61 | convolution fusion | flops 12889161728 | bytes 33816576 | tf_op jit(solution)/shard_map/cbdq,cmkb->dmqk/dot_general | solution.py:71
  1175.0 36.6 %fusion.49 = (f32[1,128,16384]{1,2,0:T(8,128)S(1)}, f32[1,128,16384]{1,2,0:T(8,128)S(1)}) fusion(f32[1,128,128,128]{1,3,2,0:T(8,128)} %copy.192, f32[1,128,128,128]{1,3,2,0:T(8,128)} %copy.191, s32[128]{0:T(128)S(1)} %iota_add_fusion.1), kind=kLoop, calls=%fused_computation.71 | loop fusion | flops 46137344 | bytes 33554944 | tf_op jit(solution)/shard_map/sub | solution.py:29
  1212.7 61.7 %copy.193 = f32[2,128,16384]{1,0,2:T(2,128)} copy(f32[2,128,16384]{1,2,0:T(8,128)S(1)} %pad_maximum_fusion.2) | data formatting | bytes 33554432 | tf_op jit(solution)/shard_map/stack | solution.py:31
  1274.5 20.2 all-to-all-start.3
  1295.1 361.8 %all-to-all-done.3 = f32[2,128,16384]{1,0,2:T(2,128)} async-done(((f32[2,128,16384]{1,0,2:T(2,128)}), f32[2,128,16384]{1,0,2:T(2,128)}, u32[]{:S(2)}, u32[]{:S(2)}) %all-to-all-start.3) | async-done | bytes 16777248 | tf_op jit(solution)/shard_map/all_to_all | solution.py:84
  1656.9 20.1 copy.247
  1677.0 21.7 fusion.74
  1709.0 28.9 %fusion.62 = f32[2,128,32,512]{3,1,2,0:T(8,128)S(1)} fusion(f32[2,32,128,512]{3,1,2,0:T(8,128)S(1)} %pad_maximum_fusion.3, f32[1,128,2,128]{1,3,2,0:T(8,128)S(1)} %get-tuple-element.28, f32[1,128,2,128]{1,3,2,0:T(8,128)S(1)} %get-tuple-element.27), kind=kOutput, calls=%fused_computation.104 | convolution fusion | flops 12884967424 | bytes 33816576 | tf_op jit(solution)/shard_map/cbdq,ckbm->dqkm/dot_general | solution.py:54
  1737.9 20.1 copy.198
  1758.0 28.6 %copy.199 = f32[2,4096,512]{2,0,1:T(2,128)} copy(f32[2,4096,512]{2,1,0:T(8,128)} %bitcast.229) | data formatting | bytes 33554432 | tf_op jit(solution)/shard_map/reshape | solution.py:57
  1786.6 19.5 all-to-all-start.4
  1806.6 362.0 %all-to-all-done.4 = f32[2,4096,512]{2,0,1:T(2,128)} async-done(((f32[2,4096,512]{2,0,1:T(2,128)}), f32[2,4096,512]{2,0,1:T(2,128)}, u32[]{:S(2)}, u32[]{:S(2)}) %all-to-all-start.4) | async-done | bytes 16777248 | tf_op jit(solution)/shard_map/all_to_all | solution.py:88
  2168.6 17.8 copy.279
  2186.4 19.2 reshape_reshape.3
  2208.6 19.7 collective-permute-done
  2240.0 50.0 %fusion = f32[2,1024,2048]{1,2,0:T(8,128)} fusion(f32[2,1024,2055]{1,2,0:T(8,128)} %maximum_bitcast_fusion, f32[1024]{0:T(1024)S(1)} %bitcast.241, f32[1024]{0:T(1024)S(1)} %bitcast.242, f32[1024]{0:T(1024)S(1)} %bitcast.236, f32[1024]{0:T(1024)S(1)} %bitcast.237, f32[1024]{0:T(1024)S(1)} %bitcast.238, f32[1024]{0:T(1024)S(1)} %bitcast.239, ...), kind=kLoop, calls=%fused_computation.2 | loop fusion | flops 62914560 | bytes 151027712 | tf_op jit(solution)/shard_map/add | solution.py:130
  2307.4 32.0 %fusion.65 = f32[2,8,128,2048]{3,1,2,0:T(8,128)} fusion(f32[2,8,128,2048]{3,2,1,0:T(8,128)} %bitcast.231, f32[1,8,2,8]{1,3,0,2:T(8,128)S(1)} %copy.167, f32[1,8,2,8]{1,3,0,2:T(8,128)S(1)} %copy.166), kind=kOutput, calls=%fused_computation.105 | convolution fusion | flops 805306624 | bytes 33555456 | tf_op jit(solution)/shard_map/cadk,cabm->dkbm/dot_general | solution.py:49
  2348.7 23.7 fusion.68
  2372.5 20.2 copy.278
  (70 shorter events, 265.8 us)
Async XLA Ops:
  24.9 368.6 %all-to-all-start = ((f32[2,128,16384]{1,0,2:T(2,128)}), f32[2,128,16384]{1,0,2:T(2,128)}, u32[]{:S(2)}, u32[]{:S(2)}) async-start(f32[2,128,16384]{1,0,2:T(2,128)} %copy.169), calls=%async_computation | async-start | bytes 33554432 | tf_op jit(solution)/shard_map/all_to_all | solution.py:84
  393.5 200.6 %all-to-all-start.2 = ((f32[32,128,512]{2,1,0:T(8,128)}), f32[32,128,512]{2,1,0:T(8,128)}, u32[]{:S(2)}, u32[]{:S(2)}) async-start(f32[32,128,512]{2,1,0:T(8,128)} %bitcast.232), calls=%async_computation.2 | async-start | bytes 16777216 | tf_op jit(solution)/shard_map/all_to_all | solution.py:107
  414.2 628.7 %copy-start = (f32[1,128,2,128]{1,3,0,2:T(8,128)}, f32[1,128,2,128]{1,3,0,2:T(8,128)S(1)}, u32[]{:S(2)}) copy-start(f32[1,128,2,128]{1,3,0,2:T(8,128)S(1)} %get-tuple-element.29) | copy-start | bytes 393220
  414.2 628.7 %copy-start.2 = (f32[1,128,2,128]{1,3,0,2:T(8,128)}, f32[1,128,2,128]{1,3,0,2:T(8,128)S(1)}, u32[]{:S(2)}) copy-start(f32[1,128,2,128]{1,3,0,2:T(8,128)S(1)} %get-tuple-element.30) | copy-start | bytes 393220
  594.1 374.9 %all-to-all-start.1 = ((f32[2,4096,512]{2,0,1:T(2,128)}), f32[2,4096,512]{2,0,1:T(2,128)}, u32[]{:S(2)}, u32[]{:S(2)}) async-start(f32[2,4096,512]{2,0,1:T(2,128)} %copy.174), calls=%async_computation.1 | async-start | bytes 33554432 | tf_op jit(solution)/shard_map/all_to_all | solution.py:88
  1274.5 382.5 %all-to-all-start.3 = ((f32[2,128,16384]{1,0,2:T(2,128)}), f32[2,128,16384]{1,0,2:T(2,128)}, u32[]{:S(2)}, u32[]{:S(2)}) async-start(f32[2,128,16384]{1,0,2:T(2,128)} %copy.193), calls=%async_computation.3 | async-start | bytes 33554432 | tf_op jit(solution)/shard_map/all_to_all | solution.py:84
  1786.6 19.9 copy-start.4
  1786.6 382.0 %all-to-all-start.4 = ((f32[2,4096,512]{2,0,1:T(2,128)}), f32[2,4096,512]{2,0,1:T(2,128)}, u32[]{:S(2)}, u32[]{:S(2)}) async-start(f32[2,4096,512]{2,0,1:T(2,128)} %copy.199), calls=%async_computation.4 | async-start | bytes 33554432 | tf_op jit(solution)/shard_map/all_to_all | solution.py:88
  2206.5 21.8 collective-permute-start
  2346.7 2.0 copy-start.1
  2346.7 2.0 copy-start.3
where the time goes:
time: 2410 us; the launch traced here: 2390 us
  waiting for transfers between devices  1390 us (58%)
  local copies, waits for them, and re-layouts  460 us (19%)
  matrix products  255 us (11%)
  other arithmetic  204 us (8%)
  starting transfers between devices  80 us (3%)
    all_to_all x2, waiting for transfers between devices, spread(): lax.all_to_all(values, ('row', 'col'), split_axis=2, concat_axis=1, tiled...  715 us
    all_to_all x2, waiting for transfers between devices, collect(): lax.all_to_all(values, ('row', 'col'), split_axis=1, concat_axis=2, tiled...  655 us
    sub x8, other arithmetic, complex_product(): real_part = values[0] * cos_part - values[1] * sin_part  128 us
    another operation x2, local copies, waits for them, and re-layouts, complex_product(): return jnp.stack([real_part, imag_part])  94 us
    dot_general x3, matrix products, dft_rows(): jnp.einsum('cbdq,ckbm->dqkm', dft_table(inner_radix, direction), partial_...  81.5 us
    dot_general x3, matrix products, dft_rows(): jnp.einsum('cadk,cabm->dkbm', dft_table(outer_radix, direction), blocked,...  75.5 us
    dot_general x2, matrix products, dft_cols(): jnp.einsum('cbdq,cmkb->dmqk', dft_table(inner_radix, direction), partial_...  63.2 us
    add x1, other arithmetic, local(): weighted + filter_taps[tap_delay][None, :, None] * turned[:, :, offset:of...  50 us
  transfers between devices with their start and end apart: 6, of which 6 were waited for; matrix products, arithmetic and copies ran while one was open for 11% of the time, Pallas kernels for 0%

commit v1 on v0

v1 whole, which is shorter than its diff:
```python
import functools
import math

import jax
import jax.numpy as jnp
import numpy as np
from jax import lax
from jax.experimental import pallas as pl
from jax.experimental.pallas import tpu as pltpu
from jax.sharding import PartitionSpec as P

AXES = ("row", "col")
LANES = 128
SPAN = 64
VMEM_LIMIT = 58 * 1024 * 1024


def times_constant(value, angle_num, angle_den, sign):
    re, im = value
    num = angle_num % angle_den
    eighth = 8 * num
    if eighth % angle_den == 0:
        octant = (eighth // angle_den) * int(sign) % 8
        root = math.sqrt(0.5)
        if octant == 0:
            return re, im
        if octant == 1:
            return (re - im) * root, (re + im) * root
        if octant == 2:
            return -im, re
        if octant == 3:
            return (re + im) * -root, (re - im) * root
        if octant == 4:
            return -re, -im
        if octant == 5:
            return (im - re) * root, (re + im) * -root
        if octant == 6:
            return im, -re
        return (re + im) * root, (im - re) * root
    turn = sign * 2.0 * math.pi * num / angle_den
    c, s = math.cos(turn), math.sin(turn)
    return re * c - im * s, re * s + im * c


def add(a, b):
    return a[0] + b[0], a[1] + b[1]


def sub(a, b):
    return a[0] - b[0], a[1] - b[1]


def dft4(x, sign):
    s0, d0 = add(x[0], x[2]), sub(x[0], x[2])
    s1, d1 = add(x[1], x[3]), sub(x[1], x[3])
    if sign < 0:
        y1 = (d0[0] + d1[1], d0[1] - d1[0])
        y3 = (d0[0] - d1[1], d0[1] + d1[0])
    else:
        y1 = (d0[0] - d1[1], d0[1] + d1[0])
        y3 = (d0[0] + d1[1], d0[1] - d1[0])
    return [add(s0, s1), y1, sub(s0, s1), y3]


def dft(x, sign):
    n = len(x)
    if n == 1:
        return x
    if n == 2:
        return [add(x[0], x[1]), sub(x[0], x[1])]
    if n == 4:
        return dft4(x, sign)
    quarter = n // 4
    parts = [dft(x[r::4], sign) for r in range(4)]
    result = [None] * n
    for k in range(quarter):
        turned = [times_constant(parts[r][k], r * k, n, sign) for r in range(4)]
        for q, value in enumerate(dft4(turned, sign)):
            result[k + q * quarter] = value
    return result


def dft_two_pass(size, sign, load, store, scratch):
    inner = min(size, 8)
    outer = size // inner
    for b in range(inner):
        values = dft([load(inner * a + b) for a in range(outer)], sign)
        for ka in range(outer):
            re, im = times_constant(values[ka], b * ka, size, sign)
            scratch[b * outer + ka, 0] = re
            scratch[b * outer + ka, 1] = im
    for ka in range(outer):
        group = [(scratch[b * outer + ka, 0], scratch[b * outer + ka, 1]) for b in range(inner)]
        for kb, value in enumerate(dft(group, sign)):
            store(ka + outer * kb, value)


def split_table(table):
    high = table.astype(jnp.bfloat16)
    low = (table - high.astype(np.float32)).astype(jnp.bfloat16)
    return high, low


def dft_matrix(size, sign, scale=1.0):
    digits = np.arange(size)
    turn = sign * 2.0 * np.pi * (digits[:, None] * digits[None, :] % size) / size
    c, s = np.cos(turn) * scale, np.sin(turn) * scale
    return np.block([[c, -s], [s, c]]).astype(np.float32)


def left_table(size, sign, scale=1.0):
    high, low = split_table(dft_matrix(size, sign, scale))
    return np.concatenate([high, high, low], axis=1)


def right_table(size, sign, scale=1.0):
    high, low = split_table(dft_matrix(size, sign, scale).T)
    return np.concatenate([high, high, low], axis=0)


def lane_twist(leads, length):
    turn = -2.0 * np.pi * (np.arange(leads)[:, None] * np.arange(LANES)[None, :] % length) / length
    return np.stack([np.cos(turn), np.sin(turn)], axis=1).astype(np.float32)


def halves(value):
    high = value.astype(jnp.bfloat16)
    low = (value - high.astype(jnp.float32)).astype(jnp.bfloat16)
    return high, low


def turn_by(re, im, c, s):
    return re * c - im * s, re * s + im * c


def turn_back(re, im, c, s):
    return re * c + im * s, im * c - re * s


def call(kernel, **options):
    cost = pl.CostEstimate(flops=options.pop("flops"), bytes_accessed=options.pop("bytes"), transcendentals=0)
    params = pltpu.CompilerParams(vmem_limit_bytes=VMEM_LIMIT)
    return pl.pallas_call(kernel, compiler_params=params, cost_estimate=cost, **options)


def deal(voltage, devices):
    rows, cols = voltage.shape[1:]
    chunks = cols // devices // LANES
    group = 4

    def kernel(x_ref, o_ref):
        for d in range(group):
            for c in range(chunks):
                at = (d * chunks + c) * LANES
                o_ref[d, c] = x_ref[:, :, at : at + LANES]

    return call(
        kernel,
        grid=(devices // group,),
        in_specs=[pl.BlockSpec((2, rows, group * chunks * LANES), lambda g: (0, 0, g))],
        out_specs=pl.BlockSpec((group, chunks, 2, rows, LANES), lambda g: (g, 0, 0, 0, 0)),
        out_shape=jax.ShapeDtypeStruct((devices, chunks, 2, rows, LANES), jnp.float32),
        flops=voltage.size,
        bytes=voltage.size * 8,
    )(voltage)


def columns_forward(values, inner_twist, twist):
    devices, chunks, _, rows, _ = values.shape
    table = jnp.asarray(left_table(rows, -1.0))
    tile = min(rows, 16)

    def kernel(x_ref, w_ref, tw_ref, t_ref, o_ref, pass_ref, mat_ref):
        def gather(step, carry):
            at = pl.ds(pl.multiple_of(step * tile, tile), tile)

            def load(s):
                return x_ref[s, 0, 0, at, :], x_ref[s, 0, 1, at, :]

            def store(k, value):
                re, im = turn_by(*value, tw_ref[0, k, at, :], tw_ref[1, k, at, :])
                lanes = slice((k % 2) * LANES, (k % 2 + 1) * LANES)
                for part, v in enumerate((re, im)):
                    high, low = halves(v)
                    for block, piece in ((part, high), (2 + part, low), (4 + part, high)):
                        rows_at = pl.ds(pl.multiple_of(block * rows + step * tile, tile), tile)
                        mat_ref[k // 2, rows_at, lanes] = piece

            dft_two_pass(devices, -1.0, load, store, pass_ref)
            return carry

        lax.fori_loop(0, rows // tile, gather, 0)

        def multiply(q, carry):
            product = jnp.dot(w_ref[...], mat_ref[q], preferred_element_type=jnp.float32)
            for h in range(2):
                lanes = slice(h * LANES, (h + 1) * LANES)
                k = 2 * q + h
                re, im = turn_by(product[:rows, lanes], product[rows:, lanes], t_ref[0, 0, k], t_ref[0, 1, k])
                o_ref[k, 0, 0] = re
                o_ref[k, 0, 1] = im
            return carry

        lax.fori_loop(0, devices // 2, multiply, 0)

    block = pl.BlockSpec((devices, 1, 2, rows, LANES), lambda c: (0, c, 0, 0, 0))
    return call(
        kernel,
        grid=(chunks,),
        in_specs=[
            block,
            pl.BlockSpec(table.shape, lambda c: (0, 0)),
            pl.BlockSpec(inner_twist.shape, lambda c: (0, 0, 0, 0)),
            pl.BlockSpec((1, 2, devices, rows, LANES), lambda c: (c, 0, 0, 0, 0)),
        ],
        out_specs=block,
        out_shape=jax.ShapeDtypeStruct(values.shape, jnp.float32),
        scratch_shapes=[
            pltpu.VMEM((devices, 2, tile, LANES), jnp.float32),
            pltpu.VMEM((devices // 2, 6 * rows, 2 * LANES), jnp.bfloat16),
        ],
        flops=values.size * 6 * rows * 2,
        bytes=values.size * 12,
    )(values, table, inner_twist, twist)


def columns_inverse(parts, inner_twist, twist, scale, first, count):
    devices = parts[0].shape[0]
    cuts = [part.shape[3] for part in parts]
    rows = sum(cuts)
    table = jnp.asarray(left_table(rows, 1.0, scale))
    tile = 8

    def kernel(*refs):
        x_refs = refs[: len(parts)]
        w_ref, tw_ref, t_ref, o_ref, mat_ref, mid_ref, pass_ref = refs[len(parts) :]

        def multiply(q, carry):
            for h in range(2):
                k = 2 * q + h
                lanes = slice(h * LANES, (h + 1) * LANES)
                at = 0
                for x_ref, cut in zip(x_refs, cuts):
                    cos_part = t_ref[0, 0, k, at : at + cut, :]
                    sin_part = t_ref[0, 1, k, at : at + cut, :]
                    turned = turn_back(x_ref[k, 0, 0], x_ref[k, 0, 1], cos_part, sin_part)
                    for part, v in enumerate(turned):
                        high, low = halves(v)
                        for piece_at, piece in ((part, high), (2 + part, low), (4 + part, high)):
                            mat_ref[piece_at * rows + at : piece_at * rows + at + cut, lanes] = piece
                    at += cut
            product = jnp.dot(w_ref[...], mat_ref[...], preferred_element_type=jnp.float32)
            for h in range(2):
                k = 2 * q + h
                lanes = slice(h * LANES, (h + 1) * LANES)
                re, im = turn_back(product[:rows, lanes], product[rows:, lanes], tw_ref[0, k], tw_ref[1, k])
                mid_ref[k, 0] = re
                mid_ref[k, 1] = im
            return carry

        lax.fori_loop(0, devices // 2, multiply, 0)

        def scatter(step, carry):
            at = pl.ds(pl.multiple_of(step * tile, tile), tile)

            def load(s):
                return mid_ref[s, 0, at, :], mid_ref[s, 1, at, :]

            def store(k, value):
                o_ref[k, 0, 0, at, :] = value[0]
                o_ref[k, 0, 1, at, :] = value[1]

            dft_two_pass(devices, 1.0, load, store, pass_ref)
            return carry

        lax.fori_loop(0, rows // tile, scatter, 0)

    def block(cut, start):
        return pl.BlockSpec((devices, 1, 2, cut, LANES), lambda c: (0, c + start, 0, 0, 0))

    size = devices * count * 2 * rows * LANES
    return call(
        kernel,
        grid=(count,),
        in_specs=[block(cut, first) for cut in cuts]
        + [
            pl.BlockSpec(table.shape, lambda c: (0, 0)),
            pl.BlockSpec(inner_twist.shape, lambda c: (0, 0, 0, 0)),
            pl.BlockSpec((1, 2, devices, rows, LANES), lambda c: (c + first, 0, 0, 0, 0)),
        ],
        out_specs=block(rows, 0),
        out_shape=jax.ShapeDtypeStruct((devices, count, 2, rows, LANES), jnp.float32),
        scratch_shapes=[
            pltpu.VMEM((6 * rows, 2 * LANES), jnp.bfloat16),
            pltpu.VMEM((devices, 2, rows, LANES), jnp.float32),
            pltpu.VMEM((devices, 2, tile, LANES), jnp.float32),
        ],
        flops=size * 6 * rows * 2,
        bytes=size * 12,
    )(*parts, table, inner_twist, twist)


def rows_filtered(values, cos_part, sin_part, first, count):
    leads = values.shape[0]
    tile = 8
    span = SPAN
    forward = jnp.asarray(right_table(LANES, -1.0))
    backward = jnp.asarray(right_table(LANES, 1.0))
    twist = jnp.asarray(lane_twist(leads, leads * LANES))
    inner = min(leads, 8)
    outer = leads // inner
    block_rows = span * tile

    def kernel(x_ref, c_ref, s_ref, f_ref, b_ref, tw_ref, o_ref, first_ref, left_ref, left2_ref, mid_ref):
        for b in range(inner):
            group = [(x_ref[inner * a + b, 0], x_ref[inner * a + b, 1]) for a in range(outer)]
            for ka, value in enumerate(dft(group, -1.0)):
                re, im = times_constant(value, b * ka, leads, -1.0)
                first_ref[b, 0, ka * tile : (ka + 1) * tile, :] = re
                first_ref[b, 1, ka * tile : (ka + 1) * tile, :] = im
        for pair in range(outer // 2):
            at = slice(pair * 2 * tile, (pair + 1) * 2 * tile)
            group = [(first_ref[b, 0, at, :], first_ref[b, 1, at, :]) for b in range(inner)]
            for kb, (re, im) in enumerate(dft(group, -1.0)):
                ka = 2 * pair + outer * kb
                c = jnp.concatenate([jnp.broadcast_to(tw_ref[ka + e, 0:1, :], (tile, LANES)) for e in range(2)], axis=0)
                s = jnp.concatenate([jnp.broadcast_to(tw_ref[ka + e, 1:2, :], (tile, LANES)) for e in range(2)], axis=0)
                re, im = turn_by(re, im, c, s)
                for part, v in enumerate((re, im)):
                    high, low = halves(v)
                    for piece_at, piece in ((part, high), (2 + part, low), (4 + part, high)):
                        left_ref[ka * tile : (ka + 2) * tile, piece_at * LANES : (piece_at + 1) * LANES] = piece

        def middle(step, carry):
            at = pl.ds(pl.multiple_of(step * block_rows, block_rows), block_rows)
            lead_at = pl.ds(pl.multiple_of(step * span, span), span)
            z = jnp.dot(left_ref[at, :], f_ref[...], preferred_element_type=jnp.float32)
            c = c_ref[lead_at].reshape(block_rows, LANES)
            s = s_ref[lead_at].reshape(block_rows, LANES)
            for part, v in enumerate(turn_by(z[:, :LANES], z[:, LANES:], c, s)):
                high, low = halves(v)
                for piece_at, piece in ((part, high), (2 + part, low), (4 + part, high)):
                    left2_ref[:, piece_at * LANES : (piece_at + 1) * LANES] = piece
            y = jnp.dot(left2_ref[...], b_ref[...], preferred_element_type=jnp.float32)
            y = y.reshape(span, tile, 2 * LANES)
            c = tw_ref[lead_at, 0:1, :]
            s = tw_ref[lead_at, 1:2, :]
            re, im = turn_back(y[:, :, :LANES], y[:, :, LANES:], c, s)
            mid_ref[lead_at, 0] = re
            mid_ref[lead_at, 1] = im
            return carry

        lax.fori_loop(0, leads // span, middle, 0)

        def load(k):
            return mid_ref[k, 0], mid_ref[k, 1]

        def store(j, value):
            o_ref[j, 0] = value[0]
            o_ref[j, 1] = value[1]

        for b in range(inner):
            group = dft([load(inner * a + b) for a in range(outer)], 1.0)
            for ka in range(outer):
                re, im = times_constant(group[ka], b * ka, leads, 1.0)
                first_ref[b, 0, ka * tile : (ka + 1) * tile, :] = re
                first_ref[b, 1, ka * tile : (ka + 1) * tile, :] = im
        for ka in range(outer):
            at = slice(ka * tile, (ka + 1) * tile)
            group = [(first_ref[b, 0, at, :], first_ref[b, 1, at, :]) for b in range(inner)]
            for kb, value in enumerate(dft(group, 1.0)):
                store(ka + outer * kb, value)

    chirp = pl.BlockSpec((leads, tile, LANES), lambda g: (0, g + first, 0))
    return call(
        kernel,
        grid=(count,),
        in_specs=[
            pl.BlockSpec((leads, 2, tile, LANES), lambda g: (0, 0, g + first, 0)),
            chirp,
            chirp,
            pl.BlockSpec(forward.shape, lambda g: (0, 0)),
            pl.BlockSpec(backward.shape, lambda g: (0, 0)),
            pl.BlockSpec(twist.shape, lambda g: (0, 0, 0)),
        ],
        out_specs=pl.BlockSpec((leads, 2, tile, LANES), lambda g: (0, 0, g, 0)),
        out_shape=jax.ShapeDtypeStruct((leads, 2, count * tile, LANES), jnp.float32),
        scratch_shapes=[
            pltpu.VMEM((inner, 2, outer * tile, LANES), jnp.float32),
            pltpu.VMEM((leads * tile, 6 * LANES), jnp.bfloat16),
            pltpu.VMEM((block_rows, 6 * LANES), jnp.bfloat16),
            pltpu.VMEM((leads, 2, tile, LANES), jnp.float32),
        ],
        flops=leads * 2 * count * tile * LANES * 6 * LANES * 4,
        bytes=leads * 2 * count * tile * LANES * 12,
    )(values, cos_part, sin_part, forward, backward, twist)


def where_lead(lead, parts):
    chunks = sum(part.shape[1] for part in parts)
    owner, chunk = lead // chunks, lead % chunks
    for number, part in enumerate(parts):
        if chunk < part.shape[1]:
            return number, owner, chunk
        chunk -= part.shape[1]


def last_frames(parts, past, pieces):
    rows = parts[0].shape[3]
    leads = sum(part.shape[0] * part.shape[1] for part in parts)
    tile = 8

    def kernel(*refs):
        o_ref = refs[-1]
        for e in range(past):
            for pa in range(pieces):
                number, owner, chunk = where_lead(leads - (past - e) * pieces + pa, parts)
                o_ref[e, pa] = refs[number][owner, chunk, :, tile - 1, :]

    def spec(part):
        return pl.BlockSpec(part.shape[:3] + (tile, LANES), lambda g: (0, 0, 0, rows // tile - 1, 0))

    return call(
        kernel,
        grid=(1,),
        in_specs=[spec(part) for part in parts],
        out_specs=pl.BlockSpec((past, pieces, 2, LANES), lambda g: (0, 0, 0, 0)),
        out_shape=jax.ShapeDtypeStruct((past, pieces, 2, LANES), jnp.float32),
        flops=leads * tile * LANES,
        bytes=leads * 2 * tile * LANES * 4,
    )(*parts)


def channelised(parts, history, filter_taps):
    rows = parts[0].shape[3]
    tap_count, channels = filter_taps.shape
    pieces = channels // LANES
    frames = sum(part.shape[0] * part.shape[1] for part in parts) // pieces
    taps = filter_taps.reshape(tap_count, pieces, LANES)
    past = tap_count - 1
    tile = 16
    table = jnp.asarray(left_table(LANES, -1.0))
    twist = jnp.asarray(lane_twist(pieces, channels))
    out_rows = tile * frames

    def kernel(*refs):
        x_refs = refs[: len(parts)]
        h_ref, taps_ref, w_ref, tw_ref, o_ref, ext_ref, last_ref, frame_ref, mat_ref, spread_ref = refs[len(parts) :]

        def at_lead(f, pa, part):
            number, owner, chunk = where_lead(f * pieces + pa, parts)
            return x_refs[number][owner, chunk, part]

        @pl.when(pl.program_id(0) == 0)
        def _():
            last_ref[...] = h_ref[...]

        first_row = lax.broadcasted_iota(jnp.int32, (tile, LANES), 0) == 0
        for e in range(past):
            for pa in range(pieces):
                for part in range(2):
                    x = at_lead(frames - past + e, pa, part)
                    before = jnp.broadcast_to(last_ref[e, pa, part : part + 1, :], (tile, LANES))
                    ext_ref[e, pa, part] = jnp.where(first_row, before, pltpu.roll(x, 1, 0))
                    last_ref[e, pa, part : part + 1, :] = x[tile - 1 : tile, :]
        for f in range(frames):
            for pa in range(pieces):
                for part in range(2):
                    ext_ref[past + f, pa, part] = at_lead(f, pa, part)

        def filtered(f, carry):
            group = []
            for pa in range(pieces):
                total = [None, None]
                for t in range(tap_count):
                    tap = taps_ref[t, pa : pa + 1, :]
                    for part in range(2):
                        term = ext_ref[f + past - t, pa, part] * tap
                        total[part] = term if total[part] is None else total[part] + term
                group.append(tuple(total))
            for ca, (re, im) in enumerate(dft(group, -1.0)):
                re, im = turn_by(re, im, tw_ref[ca, 0:1, :], tw_ref[ca, 1:2, :])
                frame_ref[ca, 0, pl.ds(f, tile, stride=frames), :] = re
                frame_ref[ca, 1, pl.ds(f, tile, stride=frames), :] = im
            return carry

        lax.fori_loop(0, frames, filtered, 0)

        for ca in range(pieces):
            for part in range(2):
                high, low = halves(frame_ref[ca, part])
                for piece_at, piece in ((part, high), (2 + part, low), (4 + part, high)):
                    mat_ref[:, piece_at * LANES : (piece_at + 1) * LANES] = piece
            y = lax.dot_general(
                w_ref[...], mat_ref[...], (((1,), (1,)), ((), ())), preferred_element_type=jnp.float32
            )
            for part in range(2):
                for h in range(out_rows // LANES):
                    block = y[part * LANES : (part + 1) * LANES, h * LANES : (h + 1) * LANES]
                    spread_ref[h, part, pl.ds(ca, LANES, stride=pieces), :] = block
        for h in range(out_rows // LANES):
            o_ref[:, :, h * LANES : (h + 1) * LANES] = spread_ref[h]

    return call(
        kernel,
        grid=(rows // tile,),
        in_specs=[pl.BlockSpec(part.shape[:3] + (tile, LANES), lambda g: (0, 0, 0, g, 0)) for part in parts]
        + [
            pl.BlockSpec(history.shape, lambda g: (0, 0, 0, 0)),
            pl.BlockSpec(taps.shape, lambda g: (0, 0, 0)),
            pl.BlockSpec(table.shape, lambda g: (0, 0)),
            pl.BlockSpec(twist.shape, lambda g: (0, 0, 0)),
        ],
        out_specs=pl.BlockSpec((2, channels, out_rows), lambda g: (0, 0, g)),
        out_shape=jax.ShapeDtypeStruct((2, channels, rows * frames), jnp.float32),
        scratch_shapes=[
            pltpu.VMEM((frames + past, pieces, 2, tile, LANES), jnp.float32),
            pltpu.VMEM(history.shape, jnp.float32),
            pltpu.VMEM((pieces, 2, out_rows, LANES), jnp.float32),
            pltpu.VMEM((out_rows, 6 * LANES), jnp.bfloat16),
            pltpu.VMEM((out_rows // LANES, 2, channels, LANES), jnp.float32),
        ],
        flops=rows * frames * channels * 2 * 6 * LANES * 2,
        bytes=rows * frames * channels * 2 * 8,
    )(*parts, history, taps, table, twist)


def exchange(values):
    return lax.all_to_all(values, AXES, split_axis=0, concat_axis=0, tiled=True)


def cut(count):
    if count == 1:
        return [(0, 1)]
    head = max(1, count // 4)
    return [(0, head), (head, count - head)]


def cos_sin(product, length, sign):
    turn = sign * 2.0 * math.pi / length * product.astype(jnp.float32)
    return jnp.stack([jnp.cos(turn), jnp.sin(turn)])


def local(voltage, chirp_phase, filter_taps):
    devices = lax.axis_size("row") * lax.axis_size("col")
    device = lax.axis_index(AXES)
    rows = voltage.shape[1]
    total_rows = rows * devices
    total_cols = voltage.shape[2]
    local_cols = total_cols // devices
    chunks = local_cols // LANES
    total = total_rows * total_cols
    leads = total_cols // LANES
    channels = filter_taps.shape[1]
    past = filter_taps.shape[0] - 1

    sent = deal(voltage, devices)
    got = exchange(sent)

    ks = jnp.arange(devices, dtype=jnp.int32)[:, None, None]
    kl = jnp.arange(rows, dtype=jnp.int32)[None, :, None]
    lane = jnp.arange(LANES, dtype=jnp.int32)[None, None, :]
    chunk = jnp.arange(chunks, dtype=jnp.int32)[:, None, None, None]
    column = device * local_cols + chunk * LANES + lane[None]
    k1 = (ks + devices * kl)[None]
    twist = jnp.moveaxis(cos_sin(k1 * column % total, total, -1.0), 0, 1)
    inner = jnp.broadcast_to(ks * kl % total_rows, (devices, rows, LANES))
    inner_twist = cos_sin(inner, total_rows, -1.0)

    phase = jnp.transpose(chirp_phase.reshape(local_cols, rows, devices), (2, 0, 1))
    phase = exchange(phase)
    phase = phase.reshape(leads, LANES, rows)
    phase = jnp.transpose(phase, (1, 2, 0))
    cos_part, sin_part = jnp.cos(phase), jnp.sin(phase)

    spread = columns_forward(got, inner_twist, twist)
    got = exchange(spread)
    got = got.reshape(leads, 2, rows, LANES)
    parts = []
    for first, count in cut(rows // 8):
        part = rows_filtered(got, cos_part, sin_part, first, count)
        parts.append(exchange(part.reshape(devices, chunks, 2, count * 8, LANES)))
    spans = []
    for first, count in cut(chunks):
        spans.append(exchange(columns_inverse(parts, inner_twist, twist, 1.0 / total, first, count)))

    route = [(d - 1, d) for d in range(1, devices)]
    history = lax.ppermute(last_frames(spans, past, channels // LANES), AXES, route)
    return channelised(spans, history, filter_taps)


def solution(mesh):
    in_specs = (P(None, AXES, None), P(AXES, None), P())
    out_specs = P(None, None, AXES)
    return jax.shard_map(local, mesh=mesh, in_specs=in_specs, out_specs=out_specs, check_vma=False)
```

time: 2410 us -> 1800 us (0.75)
  blocking collectives: 0 us -> 562 us
  waiting for transfers between devices: 1390 us -> 865 us
  local copies, waits for them, and re-layouts: 460 us -> 82 us
  matrix products: 255 us -> 0 us
  Pallas kernels: 0 us -> 187 us
  other arithmetic: 204 us -> 41.6 us
    all_to_all x0 -> x2, blocking collectives: none -> 562 us  [exchange(): return lax.all_to_all(values, AXES, split_axis=0, concat_axis=0, tiled=True)]
    all_to_all x5, waiting for transfers between devices: 1370 us -> 861 us  [exchange(): return lax.all_to_all(values, AXES, split_axis=0, concat_axis=0, tiled=True)]
    dot_general x10 -> x0, matrix products: 255 us -> none  [the longest x3 81.5 us: dft_rows(): jnp.einsum('cbdq,ckbm->dqkm', dft_table(inner_radix, direction), partial_...]
    pallas_call x0 -> x8, Pallas kernels: none -> 187 us  [the longest x2 56.3 us: rows_filtered(): call(kernel, grid=(count,), in_specs=[pl.BlockSpec((leads, 2, tile, LANES...]
    sub x8 -> x0, other arithmetic: 128 us -> none  [complex_product(): real_part = values[0] * cos_part - values[1] * sin_part]
    another operation x5 -> x0, local copies, waits for them, and re-layouts: 113 us -> none  [the longest x2 94 us: complex_product(): return jnp.stack([real_part, imag_part])]
    all_to_all x5 -> x1, local copies, waits for them, and re-layouts: 89.7 us -> 8.96 us  [exchange(): return lax.all_to_all(values, AXES, split_axis=0, concat_axis=0, tiled=True)]
    add x3, other arithmetic: 50 us -> 0.08 us  [the longest x2 0.08 us: local(): column = device * local_cols + chunk * LANES + lane[None]]
  transfers between devices with their start and end apart: 6 -> 6, of which waited for: 6 -> 6; matrix products, arithmetic and copies ran while one was open for 11% -> 7% of each run, Pallas kernels for 0% -> 6%
where the time goes in v1:
time: 1800 us
  waiting for transfers between devices  865 us (48%)
  blocking collectives  562 us (31%)
  Pallas kernels  187 us (10%)
  local copies, waits for them, and re-layouts  82 us (5%)
  starting transfers between devices  64.3 us (4%)
  other arithmetic  41.6 us (2%)
    all_to_all x5, waiting for transfers between devices, exchange(): return lax.all_to_all(values, AXES, split_axis=0, concat_axis=0, tiled=True)  861 us
    all_to_all x2, blocking collectives, exchange(): return lax.all_to_all(values, AXES, split_axis=0, concat_axis=0, tiled=True)  562 us
    all_to_all x5, starting transfers between devices, exchange(): return lax.all_to_all(values, AXES, split_axis=0, concat_axis=0, tiled=True)  62.3 us
    pallas_call x2, Pallas kernels, rows_filtered(): call(kernel, grid=(count,), in_specs=[pl.BlockSpec((leads, 2, tile, LANES...  56.3 us
    pallas_call x2, Pallas kernels, columns_inverse(): call(kernel, grid=(count,), in_specs=[block(cut, first) for cut in cuts]...  41.8 us
    sin x2, local copies, waits for them, and re-layouts, local(): cos_part, sin_part = (jnp.cos(phase), jnp.sin(phase))  40.8 us
    pallas_call x1, Pallas kernels, channelised(): call(kernel, grid=(rows // tile,), in_specs=[pl.BlockSpec(part.shape[:3]...  37.4 us
  transfers between devices with their start and end apart: 6, of which 6 were waited for; matrix products, arithmetic and copies ran while one was open for 7% of the time, Pallas kernels for 6%

profile of v1, /device:TPU:8, one launch (start us, length us, event | category | flops | bytes accessed | tf_op | source)
XLA Modules:
  0.0 1802.8 jit_solution(14082707425140869737)
XLA Ops:
  0.0 13.9 shard_map.136
  13.9 6.1 all-to-all-start
  20.0 9.0 copy.20
  29.0 11.4 copy.21
  40.4 342.1 %all-to-all-done.x_ref = f32[32,4,2,128,128]{4,3,2,1,0:T(8,128)} async-done(((f32[32,4,2,128,128]{4,3,2,1,0:T(8,128)}), f32[32,4,2,128,128]{4,3,2,1,0:T(8,128)}, u32[]{:S(2)}, u32[]{:S(2)}) %all-to-all-start) | async-done | bytes 16777248 | tf_op jit(solution)/shard_map/all_to_all | solution.py:529
  382.5 19.6 %all-to-all-start.2 = ((f32[32,512,128]{1,2,0:T(8,128)}), f32[32,512,128]{1,2,0:T(8,128)}, u32[]{:S(2)}, u32[]{:S(2)}) async-start(f32[32,512,128]{1,2,0:T(8,128)} %copy.21), calls=%async_computation.2 | async-start | bytes 16777216 | tf_op jit(solution)/shard_map/all_to_all | solution.py:529
  403.5 2.2 pad_maximum_fusion.tw_ref.refs_3_
  405.8 32.9 %fusion.4 = (f32[1,4,32,128,128]{4,3,2,0,1:T(8,128)S(1)}, f32[1,4,32,128,128]{4,3,2,0,1:T(8,128)S(1)}) fusion(s32[4,128]{1,0:T(4,128)S(1)} %iota_add_fusion.1, s32[32,128]{1,0:T(8,128)S(1)} %iota_add_fusion), kind=kLoop, calls=%fused_computation.11 | loop fusion | flops 29360128 | bytes 16795648 | tf_op jit(solution)/shard_map/cos | solution.py:541
  438.7 6.2 maximum_bitcast_fusion.t_ref.refs_4_
  444.9 35.7 %shard_map.137 = f32[32,4,2,128,128]{4,3,2,1,0:T(8,128)} custom-call(f32[32,4,2,128,128]{4,3,2,1,0:T(8,128)} %all-to-all-done.x_ref, bf16[256,768]{1,0:T(8,128)(2,1)} %constant.62.clone.w_ref.refs_4_, f32[2,32,128,128]{3,2,1,0:T(8,128)} %pad_maximum_fusion.tw_ref.refs_3_, f32[4,2,32,128,128]{4,3,2,1,0:T(8,128)} %maximum_bitcast_fusion.t_ref.refs_4_), custom_call_target="tpu_custom_call" | custom-call | flops 6442450944 | bytes 50331648 | tf_op jit(solution)/shard_map/pallas_call | solution.py:207
  480.7 102.4 %all-to-all-done.2 = f32[32,512,128]{1,2,0:T(8,128)} async-done(((f32[32,512,128]{1,2,0:T(8,128)}), f32[32,512,128]{1,2,0:T(8,128)}, u32[]{:S(2)}, u32[]{:S(2)}) %all-to-all-start.2) | async-done | bytes 8388640 | tf_op jit(solution)/shard_map/all_to_all | solution.py:529
  583.0 12.2 all-to-all-start.1
  595.3 9.0 copy.22
  604.2 31.5 %fusion.13 = (f32[32,512,128]{2,1,0:T(8,128)}, f32[32,512,128]{2,1,0:T(8,128)}) fusion(f32[32,512,128]{2,1,0:T(8,128)} %copy.22), kind=kLoop, calls=%fused_computation.28 | loop fusion | bytes 25165824 | tf_op jit(solution)/shard_map/sin | solution.py:574
  635.7 9.3 copy.23
  645.1 9.3 copy.25
  654.3 303.5 %all-to-all-done.1 = f32[32,4,2,128,128]{4,3,2,1,0:T(8,128)} async-done(((f32[32,4,2,128,128]{4,3,2,1,0:T(8,128)}), f32[32,4,2,128,128]{4,3,2,1,0:T(8,128)}, u32[]{:S(2)}, u32[]{:S(2)}) %all-to-all-start.1) | async-done | bytes 16777248 | tf_op jit(solution)/shard_map/all_to_all | solution.py:529
  957.8 15.5 shard_map.138
  973.3 19.6 %all-to-all-start.3 = ((f32[32,4,2,32,128]{4,3,2,1,0:T(8,128)}), f32[32,4,2,32,128]{4,3,2,1,0:T(8,128)}, u32[]{:S(2)}, u32[]{:S(2)}) async-start(f32[32,4,2,32,128]{4,3,2,1,0:T(8,128)} %bitcast.24), calls=%async_computation.3 | async-start | bytes 8388608 | tf_op jit(solution)/shard_map/all_to_all | solution.py:529
  992.9 40.8 %shard_map.139 = f32[128,2,96,128]{3,2,1,0:T(8,128)} custom-call(f32[128,2,128,128]{3,2,1,0:T(8,128)} %bitcast.1.x_ref, f32[128,128,128]{2,1,0:T(8,128)} %bitcast.17, f32[128,128,128]{2,1,0:T(8,128)} %bitcast.19, bf16[768,256]{1,0:T(8,128)(2,1)} %constant.63.clone.f_ref, bf16[768,256]{1,0:T(8,128)(2,1)} %constant.64.clone.b_ref, ...), custom_call_target="tpu_custom_call" | custom-call | flops 9663676416 | bytes 37748736 | tf_op jit(solution)/shard_map/pallas_call | solution.py:375
  1033.7 50.0 %all-to-all-done.3.refs_0_ = f32[32,4,2,32,128]{4,3,2,1,0:T(8,128)} async-done(((f32[32,4,2,32,128]{4,3,2,1,0:T(8,128)}), f32[32,4,2,32,128]{4,3,2,1,0:T(8,128)}, u32[]{:S(2)}, u32[]{:S(2)}) %all-to-all-start.3) | async-done | bytes 4194336 | tf_op jit(solution)/shard_map/all_to_all | solution.py:529
  1083.7 281.2 %all_to_all.35.refs_1_ = f32[32,4,2,96,128]{4,3,2,1,0:T(8,128)} all-to-all(f32[32,4,2,96,128]{4,3,2,1,0:T(8,128)} %bitcast.20), channel_id=1, replica_groups=mesh['row'=8,'col'=4] {'row','col'}, dimensions={0} | all-to-all | bytes 25165824 | tf_op jit(solution)/shard_map/all_to_all | solution.py:529
  1364.9 13.8 shard_map.140
  1378.7 4.8 all-to-all-start.5
  1383.5 27.9 %shard_map.141 = f32[32,3,2,128,128]{4,3,2,1,0:T(8,128)} custom-call(f32[32,4,2,32,128]{4,3,2,1,0:T(8,128)} %all-to-all-done.3.refs_0_, f32[32,4,2,96,128]{4,3,2,1,0:T(8,128)} %all_to_all.35.refs_1_, bf16[256,768]{1,0:T(8,128)(2,1)} %constant.66.clone.refs_2_, f32[2,32,128,128]{3,2,1,0:T(8,128)} %pad_maximum_fusion.tw_ref.refs_3_, ...), custom_call_target="tpu_custom_call" | custom-call | flops 4831838208 | bytes 37748736 | tf_op jit(solution)/shard_map/pallas_call | solution.py:282
  1411.4 62.8 %all-to-all-done.5.refs_0_ = f32[32,1,2,128,128]{4,3,2,1,0:T(8,128)} async-done(((f32[32,1,2,128,128]{4,3,2,1,0:T(8,128)}), f32[32,1,2,128,128]{4,3,2,1,0:T(8,128)}, u32[]{:S(2)}, u32[]{:S(2)}) %all-to-all-start.5) | async-done | bytes 4194336 | tf_op jit(solution)/shard_map/all_to_all | solution.py:529
  1474.2 281.2 %all_to_all.36.refs_1_ = f32[32,3,2,128,128]{4,3,2,1,0:T(8,128)} all-to-all(f32[32,3,2,128,128]{4,3,2,1,0:T(8,128)} %shard_map.141), channel_id=1, replica_groups=mesh['row'=8,'col'=4] {'row','col'}, dimensions={0} | all-to-all | bytes 25165824 | tf_op jit(solution)/shard_map/all_to_all | solution.py:529
  1755.4 1.9 shard_map.142
  1757.3 2.0 collective-permute-start
  1760.0 4.8 collective-permute-done.refs_2_
  1764.8 0.6 copy-done
  1765.5 37.4 %shard_map.143 = f32[2,1024,2048]{2,1,0:T(8,128)} custom-call(f32[32,1,2,128,128]{4,3,2,1,0:T(8,128)} %all-to-all-done.5.refs_0_, f32[32,3,2,128,128]{4,3,2,1,0:T(8,128)} %all_to_all.36.refs_1_, f32[7,8,2,128]{3,2,1,0:T(2,128)} %copy-done, f32[8,8,128]{2,1,0:T(8,128)} %bitcast.25, bf16[256,768]{1,0:T(8,128)(2,1)} %constant.62.clone.w_ref.refs_4_, ...), custom_call_target="tpu_custom_call" | custom-call | flops 6442450944 | bytes 33554432 | tf_op jit(solution)/shard_map/pallas_call | solution.py:504
  (12 shorter events, 2.1 us)
Async XLA Ops:
  13.9 368.6 %all-to-all-start = ((f32[32,4,2,128,128]{4,3,2,1,0:T(8,128)}), f32[32,4,2,128,128]{4,3,2,1,0:T(8,128)}, u32[]{:S(2)}, u32[]{:S(2)}) async-start(f32[32,4,2,128,128]{4,3,2,1,0:T(8,128)} %shard_map.136), calls=%async_computation | async-start | bytes 33554432 | tf_op jit(solution)/shard_map/all_to_all | solution.py:529
  382.5 200.6 %all-to-all-start.2 = ((f32[32,512,128]{1,2,0:T(8,128)}), f32[32,512,128]{1,2,0:T(8,128)}, u32[]{:S(2)}, u32[]{:S(2)}) async-start(f32[32,512,128]{1,2,0:T(8,128)} %copy.21), calls=%async_computation.2 | async-start | bytes 16777216 | tf_op jit(solution)/shard_map/all_to_all | solution.py:529
  583.0 374.8 %all-to-all-start.1 = ((f32[32,4,2,128,128]{4,3,2,1,0:T(8,128)}), f32[32,4,2,128,128]{4,3,2,1,0:T(8,128)}, u32[]{:S(2)}, u32[]{:S(2)}) async-start(f32[32,4,2,128,128]{4,3,2,1,0:T(8,128)} %shard_map.137), calls=%async_computation.1 | async-start | bytes 33554432 | tf_op jit(solution)/shard_map/all_to_all | solution.py:529
  973.3 110.4 %all-to-all-start.3 = ((f32[32,4,2,32,128]{4,3,2,1,0:T(8,128)}), f32[32,4,2,32,128]{4,3,2,1,0:T(8,128)}, u32[]{:S(2)}, u32[]{:S(2)}) async-start(f32[32,4,2,32,128]{4,3,2,1,0:T(8,128)} %bitcast.24), calls=%async_computation.3 | async-start | bytes 8388608 | tf_op jit(solution)/shard_map/all_to_all | solution.py:529
  1378.7 95.5 %all-to-all-start.5 = ((f32[32,1,2,128,128]{4,3,2,1,0:T(8,128)}), f32[32,1,2,128,128]{4,3,2,1,0:T(8,128)}, u32[]{:S(2)}, u32[]{:S(2)}) async-start(f32[32,1,2,128,128]{4,3,2,1,0:T(8,128)} %shard_map.140), calls=%async_computation.5 | async-start | bytes 8388608 | tf_op jit(solution)/shard_map/all_to_all | solution.py:529
  1755.4 3.9 copy-start.1
  1757.3 7.5 collective-permute-start
  1764.8 0.6 copy-start

commit v2 on v1

--- a/solution.py
+++ b/solution.py
@@ -228,12 +228,15 @@
     devices = parts[0].shape[0]
     cuts = [part.shape[3] for part in parts]
     rows = sum(cuts)
+    steps = 4
+    share = devices // steps
     table = jnp.asarray(left_table(rows, 1.0, scale))
     tile = 8
 
     def kernel(*refs):
         x_refs = refs[: len(parts)]
         w_ref, tw_ref, t_ref, o_ref, mat_ref, mid_ref, pass_ref = refs[len(parts) :]
+        base = pl.program_id(1) * share
 
         def multiply(q, carry):
             for h in range(2):
@@ -254,11 +257,11 @@
                 k = 2 * q + h
                 lanes = slice(h * LANES, (h + 1) * LANES)
                 re, im = turn_back(product[:rows, lanes], product[rows:, lanes], tw_ref[0, k], tw_ref[1, k])
-                mid_ref[k, 0] = re
-                mid_ref[k, 1] = im
+                mid_ref[base + k, 0] = re
+                mid_ref[base + k, 1] = im
             return carry
 
-        lax.fori_loop(0, devices // 2, multiply, 0)
+        lax.fori_loop(0, share // 2, multiply, 0)
 
         def scatter(step, carry):
             at = pl.ds(pl.multiple_of(step * tile, tile), tile)
@@ -273,22 +276,24 @@
             dft_two_pass(devices, 1.0, load, store, pass_ref)
             return carry
 
-        lax.fori_loop(0, rows // tile, scatter, 0)
-
-    def block(cut, start):
-        return pl.BlockSpec((devices, 1, 2, cut, LANES), lambda c: (0, c + start, 0, 0, 0))
+        @pl.when(pl.program_id(1) == steps - 1)
+        def _():
+            lax.fori_loop(0, rows // tile, scatter, 0)
+
+    def block(cut):
+        return pl.BlockSpec((share, 1, 2, cut, LANES), lambda c, s: (s, c + first, 0, 0, 0))
 
     size = devices * count * 2 * rows * LANES
     return call(
         kernel,
-        grid=(count,),
-        in_specs=[block(cut, first) for cut in cuts]
+        grid=(count, steps),
+        in_specs=[block(cut) for cut in cuts]
         + [
-            pl.BlockSpec(table.shape, lambda c: (0, 0)),
-            pl.BlockSpec(inner_twist.shape, lambda c: (0, 0, 0, 0)),
-            pl.BlockSpec((1, 2, devices, rows, LANES), lambda c: (c + first, 0, 0, 0, 0)),
-        ],
-        out_specs=block(rows, 0),
+            pl.BlockSpec(table.shape, lambda c, s: (0, 0)),
+            pl.BlockSpec((2, share, rows, LANES), lambda c, s: (0, s, 0, 0)),
+            pl.BlockSpec((1, 2, share, rows, LANES), lambda c, s: (c + first, 0, s, 0, 0)),
+        ],
+        out_specs=pl.BlockSpec((devices, 1, 2, rows, LANES), lambda c, s: (0, c, 0, 0, 0)),
         out_shape=jax.ShapeDtypeStruct((devices, count, 2, rows, LANES), jnp.float32),
         scratch_shapes=[
             pltpu.VMEM((6 * rows, 2 * LANES), jnp.bfloat16),
@@ -442,10 +447,12 @@
     table = jnp.asarray(left_table(LANES, -1.0))
     twist = jnp.asarray(lane_twist(pieces, channels))
     out_rows = tile * frames
+    pitch = frames + 1
+    unroll = 4
 
     def kernel(*refs):
         x_refs = refs[: len(parts)]
-        h_ref, taps_ref, w_ref, tw_ref, o_ref, ext_ref, last_ref, frame_ref, mat_ref, spread_ref = refs[len(parts) :]
+        h_ref, taps_ref, w_ref, tw_ref, o_ref, sum_ref, last_ref, frame_ref, mat_ref, spread_ref = refs[len(parts) :]
 
         def at_lead(f, pa, part):
             number, owner, chunk = where_lead(f * pieces + pa, parts)
@@ -456,43 +463,46 @@
             last_ref[...] = h_ref[...]
 
         first_row = lax.broadcasted_iota(jnp.int32, (tile, LANES), 0) == 0
-        for e in range(past):
-            for pa in range(pieces):
-                for part in range(2):
+        for pa in range(pieces):
+            tap = [jnp.broadcast_to(taps_ref[t, pa : pa + 1, :], (tile, LANES)) for t in range(tap_count)]
+            for part in range(2):
+                series = []
+                for e in range(past):
                     x = at_lead(frames - past + e, pa, part)
                     before = jnp.broadcast_to(last_ref[e, pa, part : part + 1, :], (tile, LANES))
-                    ext_ref[e, pa, part] = jnp.where(first_row, before, pltpu.roll(x, 1, 0))
+                    series.append(jnp.where(first_row, before, pltpu.roll(x, 1, 0)))
+                for f in range(frames):
+                    series.append(at_lead(f, pa, part))
+                    total = series[f + past] * tap[0]
+                    for t in range(1, tap_count):
+                        total = total + series[f + past - t] * tap[t]
+                    sum_ref[f, pa, part] = total
+                for e in range(past):
+                    x = at_lead(frames - past + e, pa, part)
                     last_ref[e, pa, part : part + 1, :] = x[tile - 1 : tile, :]
-        for f in range(frames):
-            for pa in range(pieces):
-                for part in range(2):
-                    ext_ref[past + f, pa, part] = at_lead(f, pa, part)
-
-        def filtered(f, carry):
-            group = []
-            for pa in range(pieces):
-                total = [None, None]
-                for t in range(tap_count):
-                    tap = taps_ref[t, pa : pa + 1, :]
-                    for part in range(2):
-                        term = ext_ref[f + past - t, pa, part] * tap
-                        total[part] = term if total[part] is None else total[part] + term
-                group.append(tuple(total))
-            for ca, (re, im) in enumerate(dft(group, -1.0)):
-                re, im = turn_by(re, im, tw_ref[ca, 0:1, :], tw_ref[ca, 1:2, :])
-                frame_ref[ca, 0, pl.ds(f, tile, stride=frames), :] = re
-                frame_ref[ca, 1, pl.ds(f, tile, stride=frames), :] = im
+
+        def pieces_dft(step, carry):
+            for u in range(unroll):
+                f = step * unroll + u
+                group = [(sum_ref[f, pa, 0], sum_ref[f, pa, 1]) for pa in range(pieces)]
+                for ca, (re, im) in enumerate(dft(group, -1.0)):
+                    re, im = turn_by(re, im, tw_ref[ca, 0:1, :], tw_ref[ca, 1:2, :])
+                    frame_ref[ca, 0, pl.ds(f, tile, stride=pitch), :] = re
+                    frame_ref[ca, 1, pl.ds(f, tile, stride=pitch), :] = im
             return carry
 
-        lax.fori_loop(0, frames, filtered, 0)
+        lax.fori_loop(0, frames // unroll, pieces_dft, 0)
 
         for ca in range(pieces):
+            slot = ca % 2
             for part in range(2):
-                high, low = halves(frame_ref[ca, part])
-                for piece_at, piece in ((part, high), (2 + part, low), (4 + part, high)):
-                    mat_ref[:, piece_at * LANES : (piece_at + 1) * LANES] = piece
+                for row in range(tile):
+                    high, low = halves(frame_ref[ca, part, row * pitch : row * pitch + frames, :])
+                    at = slice(row * frames, (row + 1) * frames)
+                    for piece_at, piece in ((part, high), (2 + part, low), (4 + part, high)):
+                        mat_ref[slot, at, piece_at * LANES : (piece_at + 1) * LANES] = piece
             y = lax.dot_general(
-                w_ref[...], mat_ref[...], (((1,), (1,)), ((), ())), preferred_element_type=jnp.float32
+                w_ref[...], mat_ref[slot], (((1,), (1,)), ((), ())), preferred_element_type=jnp.float32
             )
             for part in range(2):
                 for h in range(out_rows // LANES):
@@ -514,10 +524,10 @@
         out_specs=pl.BlockSpec((2, channels, out_rows), lambda g: (0, 0, g)),
         out_shape=jax.ShapeDtypeStruct((2, channels, rows * frames), jnp.float32),
         scratch_shapes=[
-            pltpu.VMEM((frames + past, pieces, 2, tile, LANES), jnp.float32),
+            pltpu.VMEM((frames, pieces, 2, tile, LANES), jnp.float32),
             pltpu.VMEM(history.shape, jnp.float32),
-            pltpu.VMEM((pieces, 2, out_rows, LANES), jnp.float32),
-            pltpu.VMEM((out_rows, 6 * LANES), jnp.bfloat16),
+            pltpu.VMEM((pieces, 2, tile * pitch, LANES), jnp.float32),
+            pltpu.VMEM((2, out_rows, 6 * LANES), jnp.bfloat16),
             pltpu.VMEM((out_rows // LANES, 2, channels, LANES), jnp.float32),
         ],
         flops=rows * frames * channels * 2 * 6 * LANES * 2,
@@ -529,10 +539,10 @@
     return lax.all_to_all(values, AXES, split_axis=0, concat_axis=0, tiled=True)
 
 
-def cut(count):
+def cut(count, share):
     if count == 1:
         return [(0, 1)]
-    head = max(1, count // 4)
+    head = max(1, count // share)
     return [(0, head), (head, count - head)]
 
 
@@ -577,11 +587,11 @@
     got = exchange(spread)
     got = got.reshape(leads, 2, rows, LANES)
     parts = []
-    for first, count in cut(rows // 8):
+    for first, count in cut(rows // 8, 8):
         part = rows_filtered(got, cos_part, sin_part, first, count)
         parts.append(exchange(part.reshape(devices, chunks, 2, count * 8, LANES)))
     spans = []
-    for first, count in cut(chunks):
+    for first, count in cut(chunks, 4):
         spans.append(exchange(columns_inverse(parts, inner_twist, twist, 1.0 / total, first, count)))
 
     route = [(d - 1, d) for d in range(1, devices)]

time: 1800 us -> 1790 us (level)
  waiting for transfers between devices: 865 us -> 804 us
  blocking collectives: 562 us -> 605 us
    all_to_all x5, waiting for transfers between devices: 861 us -> 799 us  [exchange(): return lax.all_to_all(values, AXES, split_axis=0, concat_axis=0, tiled=True)]
    all_to_all x2, blocking collectives: 562 us -> 605 us  [exchange(): return lax.all_to_all(values, AXES, split_axis=0, concat_axis=0, tiled=True)]
  transfers between devices with their start and end apart: 6 -> 6, of which waited for: 6 -> 5; matrix products, arithmetic and copies ran while one was open for 7% -> 7% of each run, Pallas kernels for 6% -> 6%
where the time goes in v2:
time: 1790 us
  waiting for transfers between devices  804 us (45%)
  blocking collectives  605 us (34%)
  Pallas kernels  180 us (10%)
  local copies, waits for them, and re-layouts  81.9 us (5%)
  starting transfers between devices  64.4 us (4%)
  other arithmetic  49.9 us (3%)
    all_to_all x5, waiting for transfers between devices, exchange(): return lax.all_to_all(values, AXES, split_axis=0, concat_axis=0, tiled=True)  799 us
    all_to_all x2, blocking collectives, exchange(): return lax.all_to_all(values, AXES, split_axis=0, concat_axis=0, tiled=True)  605 us
    all_to_all x5, starting transfers between devices, exchange(): return lax.all_to_all(values, AXES, split_axis=0, concat_axis=0, tiled=True)  62.4 us
    pallas_call x2, Pallas kernels, rows_filtered(): call(kernel, grid=(count,), in_specs=[pl.BlockSpec((leads, 2, tile, LANES...  56.2 us
    pallas_call x2, Pallas kernels, columns_inverse(): call(kernel, grid=(count, steps), in_specs=[block(cut) for cut in cuts] +...  42.6 us
    cos x2, other arithmetic, cos_sin(): return jnp.stack([jnp.cos(turn), jnp.sin(turn)])  41.3 us
    sin x2, local copies, waits for them, and re-layouts, local(): cos_part, sin_part = (jnp.cos(phase), jnp.sin(phase))  40.8 us
  transfers between devices with their start and end apart: 6, of which 5 were waited for; matrix products, arithmetic and copies ran while one was open for 7% of the time, Pallas kernels for 6%

profile of v2, /device:TPU:8, one launch (start us, length us, event | category | flops | bytes accessed | tf_op | source)
XLA Modules:
  0.0 1785.1 jit_solution(14392610060883584326)
XLA Ops:
  0.0 13.9 shard_map.136
  13.9 6.1 all-to-all-start
  20.0 9.0 copy.20
  29.0 11.4 copy.21
  40.4 342.1 %all-to-all-done.x_ref = f32[32,4,2,128,128]{4,3,2,1,0:T(8,128)} async-done(((f32[32,4,2,128,128]{4,3,2,1,0:T(8,128)}), f32[32,4,2,128,128]{4,3,2,1,0:T(8,128)}, u32[]{:S(2)}, u32[]{:S(2)}) %all-to-all-start) | async-done | bytes 16777248 | tf_op jit(solution)/shard_map/all_to_all | solution.py:539
  382.5 19.6 %all-to-all-start.2 = ((f32[32,512,128]{1,2,0:T(8,128)}), f32[32,512,128]{1,2,0:T(8,128)}, u32[]{:S(2)}, u32[]{:S(2)}) async-start(f32[32,512,128]{1,2,0:T(8,128)} %copy.21), calls=%async_computation.2 | async-start | bytes 16777216 | tf_op jit(solution)/shard_map/all_to_all | solution.py:539
  403.5 2.2 pad_maximum_fusion.tw_ref.refs_3_
  405.8 41.2 %fusion.4 = (f32[1,4,32,128,128]{4,3,2,0,1:T(8,128)S(1)}, f32[1,4,32,128,128]{4,3,2,0,1:T(8,128)S(1)}) fusion(s32[4,128]{1,0:T(4,128)S(1)} %iota_add_fusion.1, s32[32,128]{1,0:T(8,128)S(1)} %iota_add_fusion), kind=kLoop, calls=%fused_computation.11 | loop fusion | flops 29360128 | bytes 16795648 | tf_op jit(solution)/shard_map/cos | solution.py:551
  447.1 6.2 maximum_bitcast_fusion.t_ref.refs_4_
  453.3 35.7 %shard_map.137 = f32[32,4,2,128,128]{4,3,2,1,0:T(8,128)} custom-call(f32[32,4,2,128,128]{4,3,2,1,0:T(8,128)} %all-to-all-done.x_ref, bf16[256,768]{1,0:T(8,128)(2,1)} %constant.62.clone.w_ref.refs_4_, f32[2,32,128,128]{3,2,1,0:T(8,128)} %pad_maximum_fusion.tw_ref.refs_3_, f32[4,2,32,128,128]{4,3,2,1,0:T(8,128)} %maximum_bitcast_fusion.t_ref.refs_4_), custom_call_target="tpu_custom_call" | custom-call | flops 6442450944 | bytes 50331648 | tf_op jit(solution)/shard_map/pallas_call | solution.py:207
  489.0 94.1 %all-to-all-done.2 = f32[32,512,128]{1,2,0:T(8,128)} async-done(((f32[32,512,128]{1,2,0:T(8,128)}), f32[32,512,128]{1,2,0:T(8,128)}, u32[]{:S(2)}, u32[]{:S(2)}) %all-to-all-start.2) | async-done | bytes 8388640 | tf_op jit(solution)/shard_map/all_to_all | solution.py:539
  583.0 12.3 all-to-all-start.1
  595.3 8.9 copy.22
  604.2 31.5 %fusion.13 = (f32[32,512,128]{2,1,0:T(8,128)}, f32[32,512,128]{2,1,0:T(8,128)}) fusion(f32[32,512,128]{2,1,0:T(8,128)} %copy.22), kind=kLoop, calls=%fused_computation.28 | loop fusion | bytes 25165824 | tf_op jit(solution)/shard_map/sin | solution.py:584
  635.7 9.3 copy.23
  645.1 9.3 copy.25
  654.4 303.5 %all-to-all-done.1 = f32[32,4,2,128,128]{4,3,2,1,0:T(8,128)} async-done(((f32[32,4,2,128,128]{4,3,2,1,0:T(8,128)}), f32[32,4,2,128,128]{4,3,2,1,0:T(8,128)}, u32[]{:S(2)}, u32[]{:S(2)}) %all-to-all-start.1) | async-done | bytes 16777248 | tf_op jit(solution)/shard_map/all_to_all | solution.py:539
  957.8 9.2 shard_map.138
  967.1 19.6 %all-to-all-start.3 = ((f32[32,4,2,16,128]{4,3,2,1,0:T(8,128)}), f32[32,4,2,16,128]{4,3,2,1,0:T(8,128)S(1)}, u32[]{:S(2)}, u32[]{:S(2)}) async-start(f32[32,4,2,16,128]{4,3,2,1,0:T(8,128)} %bitcast.24), calls=%async_computation.3 | async-start | bytes 4194304 | tf_op jit(solution)/shard_map/all_to_all | solution.py:539
  986.6 46.9 %shard_map.139 = f32[128,2,112,128]{3,2,1,0:T(8,128)} custom-call(f32[128,2,128,128]{3,2,1,0:T(8,128)} %bitcast.1.x_ref, f32[128,128,128]{2,1,0:T(8,128)} %bitcast.17, f32[128,128,128]{2,1,0:T(8,128)} %bitcast.19, bf16[768,256]{1,0:T(8,128)(2,1)} %constant.63.clone.f_ref, bf16[768,256]{1,0:T(8,128)(2,1)} %constant.64.clone.b_ref, ...), custom_call_target="tpu_custom_call" | custom-call | flops 11274289152 | bytes 44040192 | tf_op jit(solution)/shard_map/pallas_call | solution.py:380
  1033.6 323.4 %all_to_all.35.refs_1_ = f32[32,4,2,112,128]{4,3,2,1,0:T(8,128)} all-to-all(f32[32,4,2,112,128]{4,3,2,1,0:T(8,128)} %bitcast.20), channel_id=1, replica_groups=mesh['row'=8,'col'=4] {'row','col'}, dimensions={0} | all-to-all | bytes 29360128 | tf_op jit(solution)/shard_map/all_to_all | solution.py:539
  1356.9 11.6 shard_map.140
  1368.5 4.8 all-to-all-start.5
  1373.4 31.0 %shard_map.141 = f32[32,3,2,128,128]{4,3,2,1,0:T(8,128)} custom-call(f32[32,4,2,16,128]{4,3,2,1,0:T(8,128)} %copy-done, f32[32,4,2,112,128]{4,3,2,1,0:T(8,128)} %all_to_all.35.refs_1_, bf16[256,768]{1,0:T(8,128)(2,1)} %constant.66.clone.refs_2_, f32[2,32,128,128]{3,2,1,0:T(8,128)} %pad_maximum_fusion.tw_ref.refs_3_, ...), custom_call_target="tpu_custom_call" | custom-call | flops 4831838208 | bytes 37748736 | tf_op jit(solution)/shard_map/pallas_call | solution.py:287
  1404.3 59.8 %all-to-all-done.5.refs_0_ = f32[32,1,2,128,128]{4,3,2,1,0:T(8,128)} async-done(((f32[32,1,2,128,128]{4,3,2,1,0:T(8,128)}), f32[32,1,2,128,128]{4,3,2,1,0:T(8,128)}, u32[]{:S(2)}, u32[]{:S(2)}) %all-to-all-start.5) | async-done | bytes 4194336 | tf_op jit(solution)/shard_map/all_to_all | solution.py:539
  1464.1 281.2 %all_to_all.36.refs_1_ = f32[32,3,2,128,128]{4,3,2,1,0:T(8,128)} all-to-all(f32[32,3,2,128,128]{4,3,2,1,0:T(8,128)} %shard_map.141), channel_id=1, replica_groups=mesh['row'=8,'col'=4] {'row','col'}, dimensions={0} | all-to-all | bytes 25165824 | tf_op jit(solution)/shard_map/all_to_all | solution.py:539
  1745.3 1.9 shard_map.142
  1747.2 2.0 collective-permute-start
  1749.2 0.6 copy.28
  1749.9 4.8 collective-permute-done.refs_2_
  1754.7 0.6 copy-done.1
  1755.3 29.8 %shard_map.143 = f32[2,1024,2048]{2,1,0:T(8,128)} custom-call(f32[32,1,2,128,128]{4,3,2,1,0:T(8,128)} %all-to-all-done.5.refs_0_, f32[32,3,2,128,128]{4,3,2,1,0:T(8,128)} %all_to_all.36.refs_1_, f32[7,8,2,128]{3,2,1,0:T(2,128)} %copy-done.1, f32[8,8,128]{2,1,0:T(8,128)} %bitcast.25, bf16[256,768]{1,0:T(8,128)(2,1)} %constant.62.clone.w_ref.refs_4_, ...), custom_call_target="tpu_custom_call" | custom-call | flops 6442450944 | bytes 33554432 | tf_op jit(solution)/shard_map/pallas_call | solution.py:514
  (14 shorter events, 1.5 us)
Async XLA Ops:
  13.9 368.6 %all-to-all-start = ((f32[32,4,2,128,128]{4,3,2,1,0:T(8,128)}), f32[32,4,2,128,128]{4,3,2,1,0:T(8,128)}, u32[]{:S(2)}, u32[]{:S(2)}) async-start(f32[32,4,2,128,128]{4,3,2,1,0:T(8,128)} %shard_map.136), calls=%async_computation | async-start | bytes 33554432 | tf_op jit(solution)/shard_map/all_to_all | solution.py:539
  382.5 200.6 %all-to-all-start.2 = ((f32[32,512,128]{1,2,0:T(8,128)}), f32[32,512,128]{1,2,0:T(8,128)}, u32[]{:S(2)}, u32[]{:S(2)}) async-start(f32[32,512,128]{1,2,0:T(8,128)} %copy.21), calls=%async_computation.2 | async-start | bytes 16777216 | tf_op jit(solution)/shard_map/all_to_all | solution.py:539
  583.0 374.8 %all-to-all-start.1 = ((f32[32,4,2,128,128]{4,3,2,1,0:T(8,128)}), f32[32,4,2,128,128]{4,3,2,1,0:T(8,128)}, u32[]{:S(2)}, u32[]{:S(2)}) async-start(f32[32,4,2,128,128]{4,3,2,1,0:T(8,128)} %shard_map.137), calls=%async_computation.1 | async-start | bytes 33554432 | tf_op jit(solution)/shard_map/all_to_all | solution.py:539
  967.1 66.5 %all-to-all-start.3 = ((f32[32,4,2,16,128]{4,3,2,1,0:T(8,128)}), f32[32,4,2,16,128]{4,3,2,1,0:T(8,128)S(1)}, u32[]{:S(2)}, u32[]{:S(2)}) async-start(f32[32,4,2,16,128]{4,3,2,1,0:T(8,128)} %bitcast.24), calls=%async_computation.3 | async-start | bytes 4194304 | tf_op jit(solution)/shard_map/all_to_all | solution.py:539
  1033.6 323.4 %copy-start = (f32[32,4,2,16,128]{4,3,2,1,0:T(8,128)}, f32[32,4,2,16,128]{4,3,2,1,0:T(8,128)S(1)}, u32[]{:S(2)}) copy-start(f32[32,4,2,16,128]{4,3,2,1,0:T(8,128)S(1)} %all-to-all-done.3.refs_0_) | copy-start | bytes 6291460
  1368.5 95.5 %all-to-all-start.5 = ((f32[32,1,2,128,128]{4,3,2,1,0:T(8,128)}), f32[32,1,2,128,128]{4,3,2,1,0:T(8,128)}, u32[]{:S(2)}, u32[]{:S(2)}) async-start(f32[32,1,2,128,128]{4,3,2,1,0:T(8,128)} %shard_map.140), calls=%async_computation.5 | async-start | bytes 8388608 | tf_op jit(solution)/shard_map/all_to_all | solution.py:539
  1745.3 3.9 copy-start.2
  1747.2 7.5 collective-permute-start
  1754.7 0.6 copy-start.1

commit v3 on v2

--- a/solution.py
+++ b/solution.py
@@ -146,7 +146,7 @@
 def deal(voltage, devices):
     rows, cols = voltage.shape[1:]
     chunks = cols // devices // LANES
-    group = 4
+    group = 8
 
     def kernel(x_ref, o_ref):
         for d in range(group):
@@ -441,14 +441,13 @@
     tap_count, channels = filter_taps.shape
     pieces = channels // LANES
     frames = sum(part.shape[0] * part.shape[1] for part in parts) // pieces
-    taps = filter_taps.reshape(tap_count, pieces, LANES)
     past = tap_count - 1
     tile = 16
-    table = jnp.asarray(left_table(LANES, -1.0))
+    table = jnp.asarray(right_table(LANES, -1.0))
     twist = jnp.asarray(lane_twist(pieces, channels))
     out_rows = tile * frames
     pitch = frames + 1
-    unroll = 4
+    together = 1
 
     def kernel(*refs):
         x_refs = refs[: len(parts)]
@@ -463,8 +462,10 @@
             last_ref[...] = h_ref[...]
 
         first_row = lax.broadcasted_iota(jnp.int32, (tile, LANES), 0) == 0
-        for pa in range(pieces):
-            tap = [jnp.broadcast_to(taps_ref[t, pa : pa + 1, :], (tile, LANES)) for t in range(tap_count)]
+
+        def fir(pa):
+            at = slice(pa * LANES, (pa + 1) * LANES)
+            tap = [jnp.broadcast_to(taps_ref[t : t + 1, at], (tile, LANES)) for t in range(tap_count)]
             for part in range(2):
                 series = []
                 for e in range(past):
@@ -481,43 +482,56 @@
                     x = at_lead(frames - past + e, pa, part)
                     last_ref[e, pa, part : part + 1, :] = x[tile - 1 : tile, :]
 
-        def pieces_dft(step, carry):
-            for u in range(unroll):
-                f = step * unroll + u
-                group = [(sum_ref[f, pa, 0], sum_ref[f, pa, 1]) for pa in range(pieces)]
+        def pieces_dft(f):
+            for first in range(0, tile, 8):
+                at = slice(first, first + 8)
+                group = [(sum_ref[f, pa, 0, at, :], sum_ref[f, pa, 1, at, :]) for pa in range(pieces)]
                 for ca, (re, im) in enumerate(dft(group, -1.0)):
-                    re, im = turn_by(re, im, tw_ref[ca, 0:1, :], tw_ref[ca, 1:2, :])
-                    frame_ref[ca, 0, pl.ds(f, tile, stride=pitch), :] = re
-                    frame_ref[ca, 1, pl.ds(f, tile, stride=pitch), :] = im
-            return carry
-
-        lax.fori_loop(0, frames // unroll, pieces_dft, 0)
-
+                    if ca > 0:
+                        re, im = turn_by(re, im, tw_ref[ca, 0:1, :], tw_ref[ca, 1:2, :])
+                    frame_ref[ca, 0, pl.ds(f + first * pitch, 8, stride=pitch), :] = re
+                    frame_ref[ca, 1, pl.ds(f + first * pitch, 8, stride=pitch), :] = im
+
+        def multiply(first):
+            rows_at = slice(first * out_rows, (first + together) * out_rows)
+            y = jnp.dot(mat_ref[rows_at, :], w_ref[...], preferred_element_type=jnp.float32)
+            for ca in range(first, first + together):
+                for part in range(2):
+                    for h in range(out_rows // LANES):
+                        at = (ca - first) * out_rows + h * LANES
+                        block = y[at : at + LANES, part * LANES : (part + 1) * LANES]
+                        spread_ref[h, part, pl.ds(ca, LANES, stride=pieces + 1), :] = jnp.transpose(block)
+
+        for pa in range(pieces):
+            fir(pa)
+        for f in range(frames):
+            pieces_dft(f)
         for ca in range(pieces):
-            slot = ca % 2
             for part in range(2):
                 for row in range(tile):
                     high, low = halves(frame_ref[ca, part, row * pitch : row * pitch + frames, :])
-                    at = slice(row * frames, (row + 1) * frames)
+                    at = slice(ca * out_rows + row * frames, ca * out_rows + (row + 1) * frames)
                     for piece_at, piece in ((part, high), (2 + part, low), (4 + part, high)):
-                        mat_ref[slot, at, piece_at * LANES : (piece_at + 1) * LANES] = piece
-            y = lax.dot_general(
-                w_ref[...], mat_ref[slot], (((1,), (1,)), ((), ())), preferred_element_type=jnp.float32
-            )
+                        mat_ref[at, piece_at * LANES : (piece_at + 1) * LANES] = piece
+            if (ca + 1) % together == 0:
+                multiply(ca + 1 - together)
+        for h in range(out_rows // LANES):
             for part in range(2):
-                for h in range(out_rows // LANES):
-                    block = y[part * LANES : (part + 1) * LANES, h * LANES : (h + 1) * LANES]
-                    spread_ref[h, part, pl.ds(ca, LANES, stride=pieces), :] = block
-        for h in range(out_rows // LANES):
-            o_ref[:, :, h * LANES : (h + 1) * LANES] = spread_ref[h]
-
+                for cb in range(LANES):
+                    tidy = spread_ref[h, part, cb * (pieces + 1) : cb * (pieces + 1) + pieces, :]
+                    o_ref[part, cb * pieces : (cb + 1) * pieces, h * LANES : (h + 1) * LANES] = tidy
+
+    tiles = rows // tile
     return call(
         kernel,
-        grid=(rows // tile,),
-        in_specs=[pl.BlockSpec(part.shape[:3] + (tile, LANES), lambda g: (0, 0, 0, g, 0)) for part in parts]
+        grid=(tiles,),
+        in_specs=[
+            pl.BlockSpec(part.shape[:3] + (tile, LANES), lambda g: (0, 0, 0, g, 0))
+            for part in parts
+        ]
         + [
             pl.BlockSpec(history.shape, lambda g: (0, 0, 0, 0)),
-            pl.BlockSpec(taps.shape, lambda g: (0, 0, 0)),
+            pl.BlockSpec(filter_taps.shape, lambda g: (0, 0)),
             pl.BlockSpec(table.shape, lambda g: (0, 0)),
             pl.BlockSpec(twist.shape, lambda g: (0, 0, 0)),
         ],
@@ -527,12 +541,12 @@
             pltpu.VMEM((frames, pieces, 2, tile, LANES), jnp.float32),
             pltpu.VMEM(history.shape, jnp.float32),
             pltpu.VMEM((pieces, 2, tile * pitch, LANES), jnp.float32),
-            pltpu.VMEM((2, out_rows, 6 * LANES), jnp.bfloat16),
-            pltpu.VMEM((out_rows // LANES, 2, channels, LANES), jnp.float32),
+            pltpu.VMEM((pieces * out_rows, 6 * LANES), jnp.bfloat16),
+            pltpu.VMEM((out_rows // LANES, 2, channels + LANES, LANES), jnp.float32),
         ],
         flops=rows * frames * channels * 2 * 6 * LANES * 2,
         bytes=rows * frames * channels * 2 * 8,
-    )(*parts, history, taps, table, twist)
+    )(*parts, history, filter_taps, table, twist)
 
 
 def exchange(values):

time: 1790 us -> 1790 us (level)
  transfers between devices with their start and end apart: 6 -> 6, of which waited for: 5 -> 5; matrix products, arithmetic and copies ran while one was open for 7% -> 8% of each run, Pallas kernels for 6% -> 6%
where the time goes in v3:
time: 1790 us; the launch traced here: 1780 us
  waiting for transfers between devices  801 us (45%)
  blocking collectives  605 us (34%)
  Pallas kernels  174 us (10%)
  local copies, waits for them, and re-layouts  81.4 us (5%)
  starting transfers between devices  64.3 us (4%)
  other arithmetic  53.3 us (3%)
    all_to_all x5, waiting for transfers between devices, exchange(): return lax.all_to_all(values, AXES, split_axis=0, concat_axis=0, tiled=True)  796 us
    all_to_all x2, blocking collectives, exchange(): return lax.all_to_all(values, AXES, split_axis=0, concat_axis=0, tiled=True)  605 us
    all_to_all x5, starting transfers between devices, exchange(): return lax.all_to_all(values, AXES, split_axis=0, concat_axis=0, tiled=True)  62.3 us
    pallas_call x2, Pallas kernels, rows_filtered(): call(kernel, grid=(count,), in_specs=[pl.BlockSpec((leads, 2, tile, LANES...  56.2 us
    cos x2, other arithmetic, cos_sin(): return jnp.stack([jnp.cos(turn), jnp.sin(turn)])  44.7 us
    pallas_call x2, Pallas kernels, columns_inverse(): call(kernel, grid=(count, steps), in_specs=[block(cut) for cut in cuts] +...  42.5 us
    sin x2, local copies, waits for them, and re-layouts, local(): cos_part, sin_part = (jnp.cos(phase), jnp.sin(phase))  40.8 us
  transfers between devices with their start and end apart: 6, of which 5 were waited for; matrix products, arithmetic and copies ran while one was open for 8% of the time, Pallas kernels for 6%

profile of v3, /device:TPU:8, one launch (start us, length us, event | category | flops | bytes accessed | tf_op | source)
XLA Modules:
  0.0 1779.9 jit_solution(18202314308197245656)
XLA Ops:
  0.0 11.5 shard_map.136
  11.5 6.1 all-to-all-start
  17.6 9.0 copy.20
  26.6 11.4 copy.21
  38.1 342.1 %all-to-all-done.x_ref = f32[32,4,2,128,128]{4,3,2,1,0:T(8,128)} async-done(((f32[32,4,2,128,128]{4,3,2,1,0:T(8,128)}), f32[32,4,2,128,128]{4,3,2,1,0:T(8,128)}, u32[]{:S(2)}, u32[]{:S(2)}) %all-to-all-start) | async-done | bytes 16777248 | tf_op jit(solution)/shard_map/all_to_all | solution.py:553
  380.1 19.6 %all-to-all-start.2 = ((f32[32,512,128]{1,2,0:T(8,128)}), f32[32,512,128]{1,2,0:T(8,128)}, u32[]{:S(2)}, u32[]{:S(2)}) async-start(f32[32,512,128]{1,2,0:T(8,128)} %copy.21), calls=%async_computation.2 | async-start | bytes 16777216 | tf_op jit(solution)/shard_map/all_to_all | solution.py:553
  400.5 0.6 broadcast_in_dim.4
  401.2 2.2 pad_maximum_fusion.tw_ref.refs_3_
  403.4 44.6 %fusion.4 = (f32[1,4,32,128,128]{4,3,2,0,1:T(8,128)S(1)}, f32[1,4,32,128,128]{4,3,2,0,1:T(8,128)S(1)}) fusion(s32[4,128]{1,0:T(4,128)S(1)} %iota_add_fusion.1, s32[32,128]{1,0:T(8,128)S(1)} %iota_add_fusion), kind=kLoop, calls=%fused_computation.11 | loop fusion | flops 29360128 | bytes 16795648 | tf_op jit(solution)/shard_map/cos | solution.py:565
  448.0 6.2 maximum_bitcast_fusion.t_ref.refs_4_
  454.3 35.7 %shard_map.137 = f32[32,4,2,128,128]{4,3,2,1,0:T(8,128)} custom-call(f32[32,4,2,128,128]{4,3,2,1,0:T(8,128)} %all-to-all-done.x_ref, bf16[256,768]{1,0:T(8,128)(2,1)} %constant.62.clone.w_ref, f32[2,32,128,128]{3,2,1,0:T(8,128)} %pad_maximum_fusion.tw_ref.refs_3_, f32[4,2,32,128,128]{4,3,2,1,0:T(8,128)} %maximum_bitcast_fusion.t_ref.refs_4_), custom_call_target="tpu_custom_call" | custom-call | flops 6442450944 | bytes 50331648 | tf_op jit(solution)/shard_map/pallas_call | solution.py:207
  490.0 90.7 %all-to-all-done.2 = f32[32,512,128]{1,2,0:T(8,128)} async-done(((f32[32,512,128]{1,2,0:T(8,128)}), f32[32,512,128]{1,2,0:T(8,128)}, u32[]{:S(2)}, u32[]{:S(2)}) %all-to-all-start.2) | async-done | bytes 8388640 | tf_op jit(solution)/shard_map/all_to_all | solution.py:553
  580.7 12.2 all-to-all-start.1
  592.9 9.0 copy.22
  601.9 31.5 %fusion.13 = (f32[32,512,128]{2,1,0:T(8,128)}, f32[32,512,128]{2,1,0:T(8,128)}) fusion(f32[32,512,128]{2,1,0:T(8,128)} %copy.22), kind=kLoop, calls=%fused_computation.27 | loop fusion | bytes 25165824 | tf_op jit(solution)/shard_map/sin | solution.py:598
  633.4 9.3 copy.23
  642.7 9.3 copy.25
  652.0 303.5 %all-to-all-done.1 = f32[32,4,2,128,128]{4,3,2,1,0:T(8,128)} async-done(((f32[32,4,2,128,128]{4,3,2,1,0:T(8,128)}), f32[32,4,2,128,128]{4,3,2,1,0:T(8,128)}, u32[]{:S(2)}, u32[]{:S(2)}) %all-to-all-start.1) | async-done | bytes 16777248 | tf_op jit(solution)/shard_map/all_to_all | solution.py:553
  955.4 9.2 shard_map.138
  964.7 19.6 %all-to-all-start.3 = ((f32[32,4,2,16,128]{4,3,2,1,0:T(8,128)}), f32[32,4,2,16,128]{4,3,2,1,0:T(8,128)S(1)}, u32[]{:S(2)}, u32[]{:S(2)}) async-start(f32[32,4,2,16,128]{4,3,2,1,0:T(8,128)} %bitcast.20), calls=%async_computation.3 | async-start | bytes 4194304 | tf_op jit(solution)/shard_map/all_to_all | solution.py:553
  984.3 46.9 %shard_map.139 = f32[128,2,112,128]{3,2,1,0:T(8,128)} custom-call(f32[128,2,128,128]{3,2,1,0:T(8,128)} %bitcast.1.x_ref, f32[128,128,128]{2,1,0:T(8,128)} %bitcast.13, f32[128,128,128]{2,1,0:T(8,128)} %bitcast.15, bf16[768,256]{1,0:T(8,128)(2,1)} %constant.63.clone.f_ref.refs_4_, bf16[768,256]{1,0:T(8,128)(2,1)} %constant.64.clone.b_ref, ...), custom_call_target="tpu_custom_call" | custom-call | flops 11274289152 | bytes 44040192 | tf_op jit(solution)/shard_map/pallas_call | solution.py:380
  1031.2 323.4 %all_to_all.35.refs_1_ = f32[32,4,2,112,128]{4,3,2,1,0:T(8,128)} all-to-all(f32[32,4,2,112,128]{4,3,2,1,0:T(8,128)} %bitcast.16), channel_id=1, replica_groups=mesh['row'=8,'col'=4] {'row','col'}, dimensions={0} | all-to-all | bytes 29360128 | tf_op jit(solution)/shard_map/all_to_all | solution.py:553
  1354.6 11.6 shard_map.140
  1366.2 4.8 all-to-all-start.5
  1371.0 30.9 %shard_map.141 = f32[32,3,2,128,128]{4,3,2,1,0:T(8,128)} custom-call(f32[32,4,2,16,128]{4,3,2,1,0:T(8,128)} %copy-done, f32[32,4,2,112,128]{4,3,2,1,0:T(8,128)} %all_to_all.35.refs_1_, bf16[256,768]{1,0:T(8,128)(2,1)} %constant.66.clone.refs_2_, f32[2,32,128,128]{3,2,1,0:T(8,128)} %pad_maximum_fusion.tw_ref.refs_3_, ...), custom_call_target="tpu_custom_call" | custom-call | flops 4831838208 | bytes 37748736 | tf_op jit(solution)/shard_map/pallas_call | solution.py:287
  1401.9 59.8 %all-to-all-done.5.refs_0_ = f32[32,1,2,128,128]{4,3,2,1,0:T(8,128)} async-done(((f32[32,1,2,128,128]{4,3,2,1,0:T(8,128)}), f32[32,1,2,128,128]{4,3,2,1,0:T(8,128)}, u32[]{:S(2)}, u32[]{:S(2)}) %all-to-all-start.5) | async-done | bytes 4194336 | tf_op jit(solution)/shard_map/all_to_all | solution.py:553
  1461.7 281.2 %all_to_all.36.refs_1_ = f32[32,3,2,128,128]{4,3,2,1,0:T(8,128)} all-to-all(f32[32,3,2,128,128]{4,3,2,1,0:T(8,128)} %shard_map.141), channel_id=1, replica_groups=mesh['row'=8,'col'=4] {'row','col'}, dimensions={0} | all-to-all | bytes 25165824 | tf_op jit(solution)/shard_map/all_to_all | solution.py:553
  1743.0 1.9 shard_map.142
  1744.8 2.0 collective-permute-start
  1746.9 5.5 collective-permute-done.refs_2_
  1752.3 0.6 copy-done.1
  1753.0 26.6 %shard_map.143 = f32[2,1024,2048]{2,1,0:T(8,128)} custom-call(f32[32,1,2,128,128]{4,3,2,1,0:T(8,128)} %all-to-all-done.5.refs_0_, f32[32,3,2,128,128]{4,3,2,1,0:T(8,128)} %all_to_all.36.refs_1_, f32[7,8,2,128]{3,2,1,0:T(2,128)} %copy-done.1, f32[8,1024]{1,0:T(8,128)} %refs_3_.1, bf16[768,256]{1,0:T(8,128)(2,1)} %constant.63.clone.f_ref.refs_4_, ...), custom_call_target="tpu_custom_call" | custom-call | flops 6442450944 | bytes 33554432 | tf_op jit(solution)/shard_map/pallas_call | solution.py:525
  (11 shorter events, 0.9 us)
Async XLA Ops:
  11.5 368.6 %all-to-all-start = ((f32[32,4,2,128,128]{4,3,2,1,0:T(8,128)}), f32[32,4,2,128,128]{4,3,2,1,0:T(8,128)}, u32[]{:S(2)}, u32[]{:S(2)}) async-start(f32[32,4,2,128,128]{4,3,2,1,0:T(8,128)} %shard_map.136), calls=%async_computation | async-start | bytes 33554432 | tf_op jit(solution)/shard_map/all_to_all | solution.py:553
  380.1 200.6 %all-to-all-start.2 = ((f32[32,512,128]{1,2,0:T(8,128)}), f32[32,512,128]{1,2,0:T(8,128)}, u32[]{:S(2)}, u32[]{:S(2)}) async-start(f32[32,512,128]{1,2,0:T(8,128)} %copy.21), calls=%async_computation.2 | async-start | bytes 16777216 | tf_op jit(solution)/shard_map/all_to_all | solution.py:553
  580.7 374.8 %all-to-all-start.1 = ((f32[32,4,2,128,128]{4,3,2,1,0:T(8,128)}), f32[32,4,2,128,128]{4,3,2,1,0:T(8,128)}, u32[]{:S(2)}, u32[]{:S(2)}) async-start(f32[32,4,2,128,128]{4,3,2,1,0:T(8,128)} %shard_map.137), calls=%async_computation.1 | async-start | bytes 33554432 | tf_op jit(solution)/shard_map/all_to_all | solution.py:553
  964.7 66.5 %all-to-all-start.3 = ((f32[32,4,2,16,128]{4,3,2,1,0:T(8,128)}), f32[32,4,2,16,128]{4,3,2,1,0:T(8,128)S(1)}, u32[]{:S(2)}, u32[]{:S(2)}) async-start(f32[32,4,2,16,128]{4,3,2,1,0:T(8,128)} %bitcast.20), calls=%async_computation.3 | async-start | bytes 4194304 | tf_op jit(solution)/shard_map/all_to_all | solution.py:553
  1031.2 323.4 %copy-start = (f32[32,4,2,16,128]{4,3,2,1,0:T(8,128)}, f32[32,4,2,16,128]{4,3,2,1,0:T(8,128)S(1)}, u32[]{:S(2)}) copy-start(f32[32,4,2,16,128]{4,3,2,1,0:T(8,128)S(1)} %all-to-all-done.3.refs_0_) | copy-start | bytes 6291460
  1366.2 95.5 %all-to-all-start.5 = ((f32[32,1,2,128,128]{4,3,2,1,0:T(8,128)}), f32[32,1,2,128,128]{4,3,2,1,0:T(8,128)}, u32[]{:S(2)}, u32[]{:S(2)}) async-start(f32[32,1,2,128,128]{4,3,2,1,0:T(8,128)} %shard_map.140), calls=%async_computation.5 | async-start | bytes 8388608 | tf_op jit(solution)/shard_map/all_to_all | solution.py:553
  1744.8 7.5 collective-permute-start
  1752.3 0.6 copy-start.1
